TPU v7x, 128 devices: a whole 4x4x4 slice. The times are simulated.
128 devices in a mesh: rep: 2 (over z_hi), shard: 64 (over y, z_lo, x, core).
Axes of the slice: x: 4, y: 4, z: 4 (z_hi: 2, z_lo: 2; z = z_hi * 2 + z_lo), core: 2. Of those that a mesh axis runs over, the one named last changes fastest.
Arguments:
- dense: bfloat16 [32768, 128], P(('rep', 'shard')), may hold values from -6 to 6
- small_ids: int32 [32768, 32], P(('rep', 'shard')), may hold values from 0 to 511
- labels: int32 [32768], P(('rep', 'shard')), may hold values 0 or 1
- small_tables: bfloat16 [32, 512, 128], replicated, may hold values from -6 to 6
- large_tables: bfloat16 [64, 8192, 128], P('shard'), may hold values from -6 to 6
- batch_sizes: int32 [64, 128], replicated, may hold values from 1 to 128, as said below
- bag_ends: int32 [64, 128, 128], P('shard'), may hold values from 0 to 256, as said below
- owner_row_index: int32 [64, 128, 256], P('shard'), may hold values from 0 to 8191
- w_first: bfloat16 [4784, 1024], replicated, may hold values from -0.09375 to 0.09375
- b_first: float32 [1024], replicated, may hold values from -3 to 3
- w_out: float32 [1024], replicated, may hold values from -0.1875 to 0.1875
Outputs:
- small_new: bfloat16 [32, 512, 128], replicated
- large_new: bfloat16 [64, 8192, 128], P('shard')
Inputs may be any that keep to these rules, and one draw needn't show every extreme that they name: `batch_sizes`: every feature has some owner, and every owner some feature, with exactly 128. `bag_ends`: nondecreasing along the last dimension; bags j >= batch_sizes[f, d] are empty; some bag list reaches 256.
All inputs are finite; a program needn't handle non-finite values. No bound on the sum of `labels` on one device may be relied on, other than what follows from the above.
Results may differ from a plain program's by a relative error of at most 0.0095.
Values may be sent and summed in bfloat16 or wider, within the bound.
A program may use at most 192 MiB of HBM per device.

v0:
```python
import jax
import jax.numpy as jnp
from jax import lax
from jax.sharding import PartitionSpec as P

step_size = 32.0


def as_sent(array):

    def short(part):
        return part.astype(jnp.bfloat16) if part.dtype == jnp.float32 else part

    return jax.tree.map(short, array)


def gathered_total(array, axis):
    return lax.all_gather(array, axis).astype(jnp.float32).sum(0)


def bag_members(limits, slot_total):
    starts = jnp.concatenate(
        [jnp.zeros(limits.shape[:-1] + (1,), jnp.int32), limits[..., :-1]], axis=-1
    )
    positions = jnp.arange(slot_total, dtype=jnp.int32)
    inside = (positions >= starts[..., None]) & (positions < limits[..., None])
    return inside.astype(jnp.bfloat16)


def silu_slope(preacts):
    squash = jax.nn.sigmoid(preacts)
    return squash * (1.0 + preacts * (1.0 - squash))


def spread_table(size_table, batch_rows, bag_span):
    chosen = jnp.arange(batch_rows, dtype=jnp.int32) * size_table[..., None] // batch_rows
    return (chosen[..., None] == jnp.arange(bag_span, dtype=jnp.int32)).astype(jnp.bfloat16)


def take_rows(table_one, row_list):
    return table_one[row_list]


def lower_pairs(gram_matrix, vec_count):
    pieces = [gram_matrix[:, index, :index] for index in range(1, vec_count)]
    return jnp.concatenate(pieces, axis=1)


def lower_square(pair_grad, vec_count):
    rows_list = []
    offset = 0
    for index in range(vec_count):
        piece = pair_grad[:, offset : offset + index]
        offset = offset + index
        rows_list.append(jnp.pad(piece, ((0, 0), (0, vec_count - index))))
    return jnp.stack(rows_list, axis=1)


def table_grads(row_list, members, gradient_list, row_total):
    slot_vectors = jnp.einsum(
        "fdks,fdke->fdse", members, gradient_list, preferred_element_type=jnp.float32
    )
    embed_width = gradient_list.shape[-1]

    def one_table(values, row_index):
        return jax.ops.segment_sum(
            values.reshape(-1, embed_width), row_index.reshape(-1), row_total
        )

    return jax.vmap(one_table)(slot_vectors, row_list)


def shards(
    dense,
    small_ids,
    labels,
    small_tables,
    large_tables,
    batch_sizes,
    bag_ends,
    owner_row_index,
    w_first,
    b_first,
    w_out,
):
    groups = lax.axis_size("shard")
    replica = lax.axis_index("rep")
    member_id = lax.axis_index("shard")
    batch_rows, embed_width = dense.shape
    owned_tables, embedding_rows = (large_tables.shape[0], large_tables.shape[1])
    small_count, small_rows = (small_tables.shape[0], small_tables.shape[1])
    feat_count = batch_sizes.shape[0]
    bag_span = bag_ends.shape[2]
    slot_total = owner_row_index.shape[2]
    pair_count = w_first.shape[0] - embed_width
    vec_count = 1 + small_count + feat_count
    first_dest = replica * groups
    own_limits = lax.dynamic_slice_in_dim(bag_ends, first_dest, groups, 1)
    own_rows = lax.dynamic_slice_in_dim(owner_row_index, first_dest, groups, 1)
    recv_sizes = lax.dynamic_slice_in_dim(batch_sizes, first_dest + member_id, 1, 1)[:, 0]
    members = bag_members(own_limits, slot_total)
    collected_rows = jax.vmap(take_rows)(large_tables, own_rows)
    pooled = jnp.einsum(
        "fdks,fdse->fdke", members, collected_rows, preferred_element_type=jnp.float32
    ).astype(jnp.bfloat16)
    arrived = lax.all_to_all(pooled, "shard", split_axis=1, concat_axis=0, tiled=True)
    recv_spread = spread_table(recv_sizes, batch_rows, bag_span)
    large_feat = jnp.einsum(
        "fbj,fje->bfe", recv_spread, arrived[:, 0], preferred_element_type=jnp.float32
    ).astype(jnp.bfloat16)
    small_hot = (small_ids[:, :, None] == jnp.arange(small_rows, dtype=jnp.int32)).astype(
        jnp.bfloat16
    )
    minor_feature = jnp.einsum(
        "btr,tre->bte", small_hot, small_tables, preferred_element_type=jnp.float32
    ).astype(jnp.bfloat16)
    vectors = jnp.concatenate([dense[:, None, :], minor_feature, large_feat], axis=1)
    gram_matrix = jnp.einsum("bie,bje->bij", vectors, vectors, preferred_element_type=jnp.float32)
    pair_values = (lower_pairs(gram_matrix, vec_count) * embed_width ** (-0.5)).astype(jnp.bfloat16)
    features = jnp.concatenate([pair_values, dense], axis=1)
    preact = jnp.dot(features, w_first, preferred_element_type=jnp.float32) + b_first
    hidden = jax.nn.silu(preact)
    logits = jnp.sum(hidden * w_out[None, :], axis=1)
    logit_grad = jax.nn.sigmoid(logits) - labels.astype(jnp.float32)
    pre_grad = (logit_grad[:, None] * w_out[None, :] * silu_slope(preact)).astype(jnp.bfloat16)
    pair_grad = jnp.einsum(
        "bh,ph->bp", pre_grad, w_first[:pair_count], preferred_element_type=jnp.float32
    ) * embed_width ** (-0.5)
    lower_part = lower_square(pair_grad, vec_count)
    symmetric = lower_part + jnp.swapaxes(lower_part, 1, 2)
    vec_grad = jnp.einsum("bij,bje->bie", symmetric, vectors.astype(jnp.float32)).astype(
        jnp.bfloat16
    )
    small_local = jnp.einsum(
        "btr,bte->tre",
        small_hot,
        vec_grad[:, 1 : 1 + small_count],
        preferred_element_type=jnp.float32,
    )
    small_sum = lax.psum(small_local, ("rep", "shard"))
    small_new = (small_tables.astype(jnp.float32) - step_size * small_sum).astype(jnp.bfloat16)
    large_grad_part = vec_grad[:, 1 + small_count :]
    folded = jnp.einsum(
        "fbj,bfe->fje", recv_spread, large_grad_part, preferred_element_type=jnp.float32
    ).astype(jnp.bfloat16)
    accumulate_gradient = lax.all_to_all(
        folded[:, None], "shard", split_axis=0, concat_axis=1, tiled=True
    )
    local_grad = table_grads(own_rows, members, accumulate_gradient, embedding_rows)
    large_grad = jax.tree.map(
        lambda part: part.astype(jnp.float32),
        jax.tree.map(lambda part: gathered_total(part, "rep"), as_sent(local_grad)),
    )
    large_new = (large_tables.astype(jnp.float32) - step_size * large_grad).astype(jnp.bfloat16)
    return (small_new, large_new)


def solution(mesh):
    placed = (
        P(("rep", "shard"), None),
        P(("rep", "shard"), None),
        P(("rep", "shard")),
        P(),
        P("shard", None, None),
        P(),
        P("shard", None, None),
        P("shard", None, None),
        P(),
        P(),
        P(),
    )
    return jax.shard_map(
        shards, mesh=mesh, in_specs=placed, out_specs=(P(), P("shard", None, None)), check_vma=False
    )
```

profile of v0, /device:TPU:1, one launch (start us, length us, event | category | flops | bytes accessed | tf_op | source)
XLA Modules:
  0.0 921.6 jit_solution(10983050159655116990)
XLA Ops:
  11.2 266.2 %gather_fusion = bf16[16384,128]{1,0:T(8,128)(2,1)} fusion(bf16[1,8192,128]{2,1,0:T(8,128)(2,1)} %param.15, s32[16384]{0:T(1024)S(1)} %bitcast.526), kind=kCustom, calls=%fused_computation | custom fusion | bytes 8519680 | tf_op jit(solution)/shard_map/vmap()/gather | solution.py:41
  277.4 6.3 convert_bitcast_fusion.2
  283.6 10.6 %all-to-all-start = ((bf16[1,64,128,128]{3,2,0,1:T(8,128)(2,1)}), bf16[1,64,128,128]{3,2,0,1:T(8,128)(2,1)S(1)}, u32[]{:S(2)}, u32[]{:S(2)}) async-start(bf16[1,64,128,128]{3,2,0,1:T(8,128)(2,1)} %convert_bitcast_fusion.2), calls=%async_computation | async-start | bytes 4194304 | tf_op jit(solution)/shard_map/all_to_all | solution.py:106
  294.6 8.1 convert_bitcast_fusion.3
  302.7 4.1 copy.345
  307.9 15.7 %all-to-all-done = bf16[1,64,128,128]{3,2,0,1:T(8,128)(2,1)S(1)} async-done(((bf16[1,64,128,128]{3,2,0,1:T(8,128)(2,1)}), bf16[1,64,128,128]{3,2,0,1:T(8,128)(2,1)S(1)}, u32[]{:S(2)}, u32[]{:S(2)}) %all-to-all-start) | async-done | bytes 2097184 | tf_op jit(solution)/shard_map/all_to_all | solution.py:106
  323.6 2.1 convert_bitcast_fusion
  325.7 4.8 pad_maximum_fusion
  330.5 10.1 %copy.346 = bf16[256,97,128]{2,1,0:T(8,128)(2,1)} copy(bf16[256,97,128]{0,2,1:T(8,128)(2,1)} %pad_maximum_fusion) | data formatting | bytes 12713984 | tf_op jit(solution)/shard_map/concatenate | solution.py:117
  340.6 13.5 %fusion.60 = f32[256,97,97]{2,1,0:T(8,128)} fusion(bf16[256,97,128]{2,1,0:T(8,128)(2,1)} %copy.346), kind=kOutput, calls=%fused_computation.184 | convolution fusion | flops 616628224 | bytes 15991808 | tf_op jit(solution)/shard_map/bie,bje->bij/dot_general | solution.py:118
  388.9 2.0 slice.808
  390.9 2.0 slice.809
  394.9 2.0 slice.811
  414.6 2.0 slice.821
  430.4 2.0 slice.829
  432.4 2.0 slice.830
  434.4 2.0 slice.831
  440.4 2.0 slice.834
  446.3 2.0 slice.837
  458.2 2.0 slice.843
  470.0 2.6 slice.849
  472.6 2.0 slice.850
  478.5 2.0 slice.853
  482.5 2.0 slice.855
  486.5 2.0 slice.857
  494.4 2.0 slice.861
  496.4 2.0 slice.862
  504.3 2.0 slice.866
  526.1 2.0 slice.877
  528.1 14.2 %concatenate.14 = f32[256,4656]{1,0:T(8,128)} concatenate(f32[256,1]{1,0:T(8,128)S(1)} %bitcast.539, f32[256,2]{1,0:T(8,128)S(1)} %bitcast.540, f32[256,3]{1,0:T(8,128)S(1)} %bitcast.541, f32[256,4]{1,0:T(8,128)S(1)} %bitcast.542, f32[256,5]{1,0:T(8,128)S(1)} %bitcast.543, f32[256,6]{1,0:T(8,128)S(1)} %bitcast.544, f32[256,7]{1,0:T(8,128)S(1)} %bitcast.545, ...), dimensions={1} | concatenate | bytes 9535488 | tf_op jit(solution)/shard_map/concatenate | solution.py:46
  542.3 2.9 multiply_convert_fusion
  545.3 6.2 multiply_reduce_fusion
  551.5 3.1 fusion.14
  627.9 15.5 %copy.443 = f32[256,97,97]{1,0,2:T(8,128)} copy(f32[256,97,97]{2,0,1:T(8,128)} %constant_dynamic-update-slice_fusion) | data formatting | bytes 19269632 | tf_op jit(solution)/shard_map/stack | solution.py:56
  643.5 12.3 %bitcast_add_fusion = bf16[256,97,97]{2,0,1:T(8,128)(2,1)} fusion(f32[256,97,97]{2,0,1:T(8,128)} %constant_dynamic-update-slice_fusion, f32[256,97,97]{1,0,2:T(8,128)} %copy.443), kind=kLoop, calls=%fused_computation.7 | loop fusion | flops 4817408 | bytes 24087040 | tf_op jit(solution)/shard_map/add | solution.py:130
  655.8 12.3 %fusion.11 = bf16[256,97,128]{2,1,0:T(8,128)(2,1)} fusion(bf16[256,97,128]{2,1,0:T(8,128)(2,1)S(1)} %bitcast.528, bf16[256,97,97]{2,0,1:T(8,128)(2,1)} %bitcast_add_fusion), kind=kOutput, calls=%fused_computation.20 | convolution fusion | flops 616628224 | bytes 17531392 | tf_op jit(solution)/shard_map/bij,bje->bie/dot_general | solution.py:131
  668.1 2.9 slice.981
  671.0 6.3 fusion
  677.4 5.1 slice.982
  682.5 5.9 convert_bitcast_fusion.1
  688.4 4.7 all-to-all-start.1
  693.9 33.0 %all-to-all-done.1 = bf16[64,1,128,128]{3,2,1,0:T(8,128)(2,1)S(1)} async-done(((bf16[64,1,128,128]{3,2,1,0:T(8,128)(2,1)}), bf16[64,1,128,128]{3,2,1,0:T(8,128)(2,1)S(1)}, u32[]{:S(2)}, u32[]{:S(2)}) %all-to-all-start.1) | async-done | bytes 2097184 | tf_op jit(solution)/shard_map/all_to_all | solution.py:146
  726.9 5.0 fusion.17
  731.9 90.0 %scatter_custom_fusion = f32[8192,128]{1,0:T(8,128)} fusion(s32[16384]{0:T(1024)S(1)} %broadcast_select_fusion, f32[16384,128]{1,0:T(8,128)} %bitcast.529, f32[]{:T(128)} %constant.16.clone.1), kind=kCustom, calls=%fused_computation.43 | custom fusion | flops 2097152 | bytes 4194816
  821.9 3.7 convert_element_type.266
  825.6 74.9 %all-reduce.98.cloned.1.call-done = f32[32,512,128]{2,1,0:T(8,128)} async-done(((f32[32,512,128]{2,1,0:T(8,128)}), f32[32,512,128]{2,1,0:T(8,128)}) %all-reduce.98.cloned.1.call-update) | async-done | bytes 8388624 | tf_op jit(solution)/shard_map/psum | solution.py:140
  900.5 8.0 subtract_convert_fusion
  908.6 3.4 convert_reduce_fusion
  (331 shorter events, 215.2 us)
Async XLA Ops:
  8.0 298.9 %copy-start = (s32[64,128]{1,0:T(8,128)S(1)}, s32[64,128]{1,0:T(8,128)}, u32[]{:S(2)}) copy-start(s32[64,128]{1,0:T(8,128)} %param.16) | copy-start | bytes 98308
  9.6 267.8 %copy-start.4 = (s32[64,128]{1,0:T(8,128)}, s32[64,128]{1,0:T(8,128)S(1)}, u32[]{:S(2)}) copy-start(s32[64,128]{1,0:T(8,128)S(1)} %get-tuple-element.7) | copy-start | bytes 98308
  277.4 17.2 %copy-start.11 = (s32[256,32]{0,1:T(8,128)S(1)}, s32[256,32]{0,1:T(8,128)}, u32[]{:S(2)}) copy-start(s32[256,32]{0,1:T(8,128)} %param.12) | copy-start | bytes 98308
  283.6 23.2 %copy-start.6 = (bf16[256,128]{1,0:T(8,128)(2,1)S(1)}, bf16[256,128]{1,0:T(8,128)(2,1)}, u32[]{:S(2)}) copy-start(bf16[256,128]{1,0:T(8,128)(2,1)} %param.11) | copy-start | bytes 196612
  283.6 39.9 %all-to-all-start = ((bf16[1,64,128,128]{3,2,0,1:T(8,128)(2,1)}), bf16[1,64,128,128]{3,2,0,1:T(8,128)(2,1)S(1)}, u32[]{:S(2)}, u32[]{:S(2)}) async-start(bf16[1,64,128,128]{3,2,0,1:T(8,128)(2,1)} %convert_bitcast_fusion.2), calls=%async_computation | async-start | bytes 4194304 | tf_op jit(solution)/shard_map/all_to_all | solution.py:106
  294.2 606.3 %all-reduce.98.cloned.1.call-start = ((), (), s32[]{:S(2)}) async-start(), calls=%async_computation.2 | async-start | bytes 16777216 | tf_op jit(solution)/shard_map/psum | solution.py:140
  524.1 21.1 %copy-start.13 = (f32[1024]{0:T(1024)S(1)}, f32[1024]{0:T(1024)}, u32[]{:S(2)}) copy-start(f32[1024]{0:T(1024)} %param.20) | copy-start | bytes 12292
  524.1 21.1 %copy-start.14 = (f32[1024]{0:T(1024)S(1)}, f32[1024]{0:T(1024)}, u32[]{:S(2)}) copy-start(f32[1024]{0:T(1024)} %param.21) | copy-start | bytes 12292
  542.3 9.2 slice-start.2
  545.2 6.2 copy-start.7
  545.3 6.3 slice-start.3
  545.3 6.3 slice-start.4
  554.6 9.9 %copy-start.10 = (pred[97]{0:T(512)(128)(4,1)S(1)}, pred[97]{0:T(512)(128)(4,1)}, u32[]{:S(2)}) copy-start(pred[97]{0:T(512)(128)(4,1)} %constant.17.clone.1) | copy-start | bytes 295
  627.9 27.8 %slice-start = ((s8[6815744]{0:T(1024)(128)(4,1)}), s8[2621440]{0:T(1024)(128)(4,1)S(1)}, s32[]{:S(2)}) async-start(s8[6815744]{0:T(1024)(128)(4,1)} %bitcast.527), calls=%async_computation.4 | async-start | bytes 5242880
  643.5 12.3 %slice-start.1 = ((s8[6815744]{0:T(1024)(128)(4,1)}), s8[4194304]{0:T(1024)(128)(4,1)S(1)}, s32[]{:S(2)}) async-start(s8[6815744]{0:T(1024)(128)(4,1)} %bitcast.527), calls=%async_computation.5 | async-start | bytes 8388608
  655.8 15.2 %copy-start.12 = (s32[256,32]{0,1:T(8,128)S(1)}, s32[256,32]{0,1:T(8,128)}, u32[]{:S(2)}) copy-start(s32[256,32]{0,1:T(8,128)} %param.12) | copy-start | bytes 98308
  677.3 15.8 %copy-start.3 = (s32[1,64,256]{2,1,0:T(8,128)S(1)}, s32[1,64,256]{2,1,0:T(8,128)}, u32[]{:S(2)}) copy-start(s32[1,64,256]{2,1,0:T(8,128)} %get-tuple-element.3) | copy-start | bytes 196612
  677.4 15.9 %copy-start.9 = (s32[2]{0:T(128)S(1)}, s32[2]{0:T(128)}, u32[]{:S(2)}) copy-start(s32[2]{0:T(128)} %constant.246) | copy-start | bytes 28
  677.4 16.2 %copy-start.8 = (s32[2]{0:T(128)S(1)}, s32[2]{0:T(128)}, u32[]{:S(2)}) copy-start(s32[2]{0:T(128)} %constant.249) | copy-start | bytes 28
  677.4 49.5 %copy-start.5 = (s32[64,128]{1,0:T(8,128)S(1)}, s32[64,128]{1,0:T(8,128)}, u32[]{:S(2)}) copy-start(s32[64,128]{1,0:T(8,128)} %copy-done.4) | copy-start | bytes 98308
  688.4 38.4 %all-to-all-start.1 = ((bf16[64,1,128,128]{3,2,1,0:T(8,128)(2,1)}), bf16[64,1,128,128]{3,2,1,0:T(8,128)(2,1)S(1)}, u32[]{:S(2)}, u32[]{:S(2)}) async-start(bf16[64,1,128,128]{3,2,1,0:T(8,128)(2,1)} %convert_bitcast_fusion.1), calls=%async_computation.1 | async-start | bytes 4194304 | tf_op jit(solution)/shard_map/all_to_all | solution.py:146
  693.1 215.4 %all-gather.3.cloned.1.call-start = ((), (), s32[]{:S(2)}) async-start(), calls=%async_computation.3 | async-start | bytes 6291456 | tf_op jit(solution)/shard_map/all_gather | solution.py:18
  825.6 86.3 %copy-start.2 = (bf16[1,8192,128]{2,1,0:T(8,128)(2,1)S(1)}, bf16[1,8192,128]{2,1,0:T(8,128)(2,1)}, u32[]{:S(2)}) copy-start(bf16[1,8192,128]{2,1,0:T(8,128)(2,1)} %param.15) | copy-start | bytes 6291460
  825.6 88.3 %copy-start.1 = (s32[64,128]{1,0:T(8,128)S(1)}, s32[64,128]{1,0:T(8,128)}, u32[]{:S(2)}) copy-start(s32[64,128]{1,0:T(8,128)} %param.16) | copy-start | bytes 98308
Sparse Core Ops, SparseCore 0:
  677.5 223.0 all-reduce.97
Sparse Core Ops, SparseCore 1:
  825.7 61.4 all-gather.2
where the time goes:
time: 932 us; the launch traced here: 922 us
  local copies, waits for them, and re-layouts  567 us (61%)
  other arithmetic  130 us (14%)
  waiting for transfers between devices  124 us (13%)
  matrix products  68.6 us (7%)
  between operations  17 us (2%)
  starting transfers between devices  15.7 us (2%)
    gather x2, local copies, waits for them, and re-layouts, take_rows(): return table_one[row_list]  266 us
    slice x96, local copies, waits for them, and re-layouts, lower_pairs(): pieces = [gram_matrix[:, index, :index] for index in range(1, vec_count)]  174 us
    unnamed x8, other arithmetic  91.3 us
    psum x1, waiting for transfers between devices, shards(): small_sum = lax.psum(small_local, ('rep', 'shard'))  74.9 us
    unnamed x137, local copies, waits for them, and re-layouts  63 us
    all_to_all x1, waiting for transfers between devices, shards(): lax.all_to_all(folded[:, None], 'shard', split_axis=0, concat_axis=1, til...  33 us
  transfers between devices with their start and end apart: 4, of which 3 were waited for; matrix products, arithmetic and copies ran while one was open for 14% of the time, Pallas kernels for 0%

commit v1 on v0

v1 whole, which is shorter than its diff:
```python
import functools
import jax
import jax.numpy as jnp
from jax import lax
from jax.experimental import pallas as pl
from jax.experimental.pallas import tpu as pltpu
from jax.sharding import Mesh, PartitionSpec as P

step_size = 32.0
LANES = 128
VMEM_CAP = 67_000_000
F32 = jnp.float32
BF16 = jnp.bfloat16

OWNERS = ("y", "zl", "x", "core")
ALL = ("rep",) + OWNERS
PLANE = ("rep", "y", "zl", "core")


def whole(space=pltpu.VMEM):
    return pl.BlockSpec(memory_space=space)


def bag_mask(ends_row, slots):
    bags = ends_row.shape[1]
    lane = lax.broadcasted_iota(jnp.int32, (1, bags), 1)
    starts = jnp.where(lane == 0, 0, pltpu.roll(ends_row, 1, 1))
    slot = lax.broadcasted_iota(jnp.int32, (slots, bags), 0)
    inside = (slot >= starts) & (slot < ends_row)
    return jnp.where(inside, 1.0, 0.0).astype(BF16)


def pool_kernel(ids, used, ends, table, out, wide, rows, *, group, unroll):
    dests, bags = ends.shape
    slots = ids.shape[1]
    wide[...] = table[...].astype(F32)
    rows[...] = jnp.zeros(rows.shape, F32)

    def one_group(g, _):
        def one_dest(i, _):
            d = g * group + i
            base = i * slots

            def chunk(c, _):
                first = c * unroll
                for u in range(unroll):
                    rows[pl.ds(base + first + u, 1), :] = wide[pl.ds(ids[d, first + u], 1), :]
                return 0

            lax.fori_loop(0, (used[d] + unroll - 1) // unroll, chunk, 0)
            return 0

        lax.fori_loop(0, group, one_dest, 0)
        limits = ends[pl.ds(pl.multiple_of(g * group, group), group), :]
        for i in range(group):
            mask = bag_mask(limits[i : i + 1], slots)
            taken = rows[i * slots : (i + 1) * slots, :].astype(BF16)
            total = lax.dot_general(
                mask, taken, (((0,), (0,)), ((), ())), preferred_element_type=F32
            )
            out[g * group + i] = total.astype(BF16)
        return 0

    lax.fori_loop(0, dests // group, one_group, 0)


def pool(ids, used, ends, table):
    dests, bags = ends.shape
    slots = ids.shape[1]
    group = 8
    return pl.pallas_call(
        functools.partial(pool_kernel, group=group, unroll=16),
        out_shape=jax.ShapeDtypeStruct((dests, bags, LANES), BF16),
        in_specs=[whole(pltpu.SMEM), whole(pltpu.SMEM), whole(), whole()],
        out_specs=whole(),
        scratch_shapes=[
            pltpu.VMEM(table.shape, F32),
            pltpu.VMEM((group * slots, LANES), F32),
        ],
        compiler_params=pltpu.CompilerParams(vmem_limit_bytes=VMEM_CAP),
        name="pool",
    )(ids, used, ends, table)


def scatter_kernel(ids, used, ends, folds, table, out, vals, *accs, group, unroll):
    dests, bags = ends.shape
    slots = ids.shape[1]
    ways = len(accs)
    for acc in accs:
        acc[...] = jnp.zeros(acc.shape, F32)

    def one_group(g, _):
        limits = ends[pl.ds(pl.multiple_of(g * group, group), group), :]
        for i in range(group):
            mask = bag_mask(limits[i : i + 1], slots)
            vals[i * slots : (i + 1) * slots, :] = jnp.dot(
                mask, folds[g * group + i], preferred_element_type=F32
            )

        def one_dest(i, _):
            d = g * group + i
            base = i * slots

            def chunk(c, _):
                first = c * unroll
                for v in range(0, unroll, ways):
                    spots = [ids[d, first + v + w] for w in range(ways)]
                    sums = [
                        accs[w][pl.ds(spots[w], 1), :] + vals[pl.ds(base + first + v + w, 1), :]
                        for w in range(ways)
                    ]
                    for w in range(ways):
                        accs[w][pl.ds(spots[w], 1), :] = sums[w]
                return 0

            lax.fori_loop(0, (used[d] + unroll - 1) // unroll, chunk, 0)
            return 0

        lax.fori_loop(0, group, one_dest, 0)
        return 0

    lax.fori_loop(0, dests // group, one_group, 0)

    def finish(c, _):
        span = pl.ds(pl.multiple_of(c * 128, 128), 128)
        total = accs[0][span, :]
        for acc in accs[1:]:
            total = total + acc[span, :]
        out[span, :] = (table[span, :].astype(F32) - step_size * total).astype(BF16)
        return 0

    lax.fori_loop(0, table.shape[0] // 128, finish, 0)


def scatter(ids, used, ends, folds, table, ways=4):
    slots = ids.shape[1]
    group = 8
    return pl.pallas_call(
        functools.partial(scatter_kernel, group=group, unroll=16),
        out_shape=jax.ShapeDtypeStruct(table.shape, BF16),
        in_specs=[whole(pltpu.SMEM), whole(pltpu.SMEM), whole(), whole(), whole()],
        out_specs=whole(),
        scratch_shapes=[pltpu.VMEM((group * slots, LANES), F32)]
        + [pltpu.VMEM(table.shape, F32)] * ways,
        compiler_params=pltpu.CompilerParams(vmem_limit_bytes=VMEM_CAP),
        name="scatter",
    )(ids, used, ends, folds, table)


def top_kernel(
    sizes, arrived, small, dense, labels, w_first, b_first, w_out,
    small_out, fold_out,
    vec, gram, feats, preact, pre_grad, pair_grad,
    *, pitch, vec_count,
):
    feat_count, bags, width = arrived.shape
    small_count, batch, _ = small.shape
    shift = batch.bit_length() - 1
    pairs = vec_count * (vec_count - 1) // 2
    scale = width ** (-0.5)
    hidden = w_first.shape[1]
    first_large = 1 + small_count

    def column(row, count=batch, first=0):
        return pl.ds(first * pitch + row, count, stride=pitch)

    for row in range(vec_count, pitch):
        vec[column(row), :] = jnp.zeros((batch, width), F32)
    vec[batch * pitch :, :] = jnp.zeros((vec.shape[0] - batch * pitch, width), F32)
    vec[column(0), :] = dense[...].astype(F32)
    for t in range(small_count):
        vec[column(1 + t), :] = small[t].astype(F32)
    sample = lax.broadcasted_iota(jnp.int32, (batch, bags), 0)
    bag = lax.broadcasted_iota(jnp.int32, (batch, bags), 1)
    for f in range(feat_count):
        hot = jnp.where(((sample * sizes[f]) >> shift) == bag, 1.0, 0.0).astype(BF16)
        vec[column(first_large + f), :] = jnp.dot(hot, arrived[f], preferred_element_type=F32)

    together = 8

    def gram_step(s, _):
        base = s * (together * pitch)
        blocks = [
            vec[pl.ds(pl.multiple_of(base + n * pitch, 8), pitch), :].astype(BF16)
            for n in range(together)
        ]
        for n in range(together):
            g = lax.dot_general(
                blocks[n], blocks[n], (((1,), (1,)), ((), ())), preferred_element_type=F32
            )
            gram[pl.ds(pl.multiple_of(base + n * pitch, 8), pitch), 0:pitch] = g * scale
        return 0

    lax.fori_loop(0, batch // together, gram_step, 0)

    part = 64
    lane = lax.broadcasted_iota(jnp.int32, (part, LANES), 1)

    def pack_step(s, _):
        rows = pl.ds(pl.multiple_of(s * part, part), part)
        tile = None
        offset = 0
        for i in range(1, vec_count + 1):
            if i < vec_count:
                piece = gram[pl.ds(s * (part * pitch) + i, part, stride=pitch), :]
                length = i
            else:
                piece = dense[rows, :].astype(F32)
                length = width
            turn = offset % LANES
            number = offset // LANES
            if turn:
                piece = pltpu.roll(piece, turn, 1)
                tile = jnp.where(lane >= turn, piece, tile)
            else:
                tile = piece
            offset += length
            if offset // LANES > number:
                feats[rows, number * LANES : (number + 1) * LANES] = tile.astype(BF16)
                tile = piece
        if offset % LANES:
            number = offset // LANES
            feats[rows, number * LANES : (number + 1) * LANES] = tile.astype(BF16)
        return 0

    lax.fori_loop(0, batch // part, pack_step, 0)

    depth = pairs + width
    bulk = depth // LANES * LANES
    wide = 256
    for n in range(0, hidden, wide):
        total = jnp.dot(feats[:, :bulk], w_first[:bulk, n : n + wide], preferred_element_type=F32)
        total = total + jnp.dot(
            feats[:, bulk:depth], w_first[bulk:depth, n : n + wide], preferred_element_type=F32
        )
        preact[:, n : n + wide] = total + b_first[:, n : n + wide]

    def head_step(s, _):
        rows = pl.ds(pl.multiple_of(s * 16, 16), 16)
        v = preact[rows, :]
        squash = jax.nn.sigmoid(v)
        logit = jnp.sum(v * squash * w_out[...], axis=1, keepdims=True)
        logit_grad = jax.nn.sigmoid(logit) - labels[rows, :].astype(F32)
        slope = squash * (1.0 + v * (1.0 - squash))
        pre_grad[rows, :] = (logit_grad * w_out[...] * slope).astype(BF16)
        return 0

    lax.fori_loop(0, batch // 16, head_step, 0)

    bulk = pairs // wide * wide
    for n in range(0, pairs, wide):
        span = min(wide, pairs - n)
        g = lax.dot_general(
            pre_grad[...], w_first[n : n + span, :], (((1,), (1,)), ((), ())),
            preferred_element_type=F32,
        )
        pair_grad[:, n : n + span] = g * scale

    def unpack_step(s, _):
        rows = pl.ds(pl.multiple_of(s * part, part), part)
        offset = 0
        for i in range(pitch):
            where_to = pl.ds(s * (part * pitch) + i, part, stride=pitch)
            if i == 0 or i >= vec_count:
                gram[where_to, :] = jnp.zeros((part, LANES), F32)
                continue
            turn = offset % LANES
            number = offset // LANES
            back = (LANES - turn) % LANES
            piece = pair_grad[rows, number * LANES : (number + 1) * LANES]
            if back:
                piece = pltpu.roll(piece, back, 1)
            if turn + i > LANES:
                more = pair_grad[rows, (number + 1) * LANES : (number + 2) * LANES]
                piece = jnp.where(lane < LANES - turn, piece, pltpu.roll(more, back, 1))
            gram[where_to, :] = jnp.where(lane < i, piece, 0.0)
            offset += i
        return 0

    lax.fori_loop(0, batch // part, unpack_step, 0)

    def grad_step(s, _):
        base = s * (together * pitch)
        found = []
        for n in range(together):
            spot = pl.multiple_of(base + n * pitch, 8)
            lower = gram[pl.ds(spot, pitch), :].astype(BF16)
            vectors = vec[pl.ds(spot, LANES), :].astype(BF16)
            found.append((lower, vectors))
        for n in range(together):
            lower, vectors = found[n]
            spot = pl.multiple_of(base + n * pitch, 8)
            one = jnp.dot(lower, vectors, preferred_element_type=F32)
            two = lax.dot_general(
                lower, vectors[:pitch], (((0,), (0,)), ((), ())), preferred_element_type=F32
            )
            vec[pl.ds(spot, pitch), :] = one + two[:pitch]
        return 0

    lax.fori_loop(0, batch // together, grad_step, 0)

    for t in range(small_count):
        small_out[t] = vec[column(1 + t), :].astype(BF16)
    sample_t = lax.broadcasted_iota(jnp.int32, (bags, batch), 1)
    bag_t = lax.broadcasted_iota(jnp.int32, (bags, batch), 0)
    for f in range(feat_count):
        hot = jnp.where(((sample_t * sizes[f]) >> shift) == bag_t, 1.0, 0.0).astype(BF16)
        grads = vec[column(first_large + f), :].astype(BF16)
        fold = jnp.dot(hot, grads, preferred_element_type=F32).astype(BF16)
        for copy in range(fold_out.shape[0]):
            fold_out[copy, f] = fold


def top(sizes, arrived, small, dense, labels, w_first, b_first, w_out, copies):
    feat_count, bags, width = arrived.shape
    small_count, batch, _ = small.shape
    vec_count = 1 + small_count + feat_count
    pitch = -(-vec_count // 8) * 8
    pairs = vec_count * (vec_count - 1) // 2
    depth = pairs + width
    hidden = w_first.shape[1]

    def up(n):
        return -(-n // LANES) * LANES

    return pl.pallas_call(
        functools.partial(top_kernel, pitch=pitch, vec_count=vec_count),
        out_shape=(
            jax.ShapeDtypeStruct((small_count, batch, width), BF16),
            jax.ShapeDtypeStruct((copies, feat_count, bags, width), BF16),
        ),
        in_specs=[whole(pltpu.SMEM)] + [whole()] * 7,
        out_specs=(whole(), whole()),
        scratch_shapes=[
            pltpu.VMEM((batch * pitch + LANES - pitch, width), F32),
            pltpu.VMEM((batch * pitch, LANES), F32),
            pltpu.VMEM((batch, up(depth)), BF16),
            pltpu.VMEM((batch, hidden), F32),
            pltpu.VMEM((batch, hidden), BF16),
            pltpu.VMEM((batch, up(pairs)), F32),
        ],
        compiler_params=pltpu.CompilerParams(vmem_limit_bytes=VMEM_CAP),
        name="top",
    )(sizes, arrived, small, dense, labels, w_first, b_first, w_out)


def shards(
    dense, small_ids, labels, small_tables, large_tables,
    batch_sizes, bag_ends, owner_row_index, w_first, b_first, w_out,
):
    groups = 1
    for name in OWNERS:
        groups = groups * lax.axis_size(name)
    copies = lax.axis_size("rep")
    replica = lax.axis_index("rep")
    me = lax.axis_index(ALL)
    first = replica * groups
    small_rows = small_tables.shape[1]
    table = large_tables[0]
    ends, ids = bag_ends[0], owner_row_index[0]
    used = ends[:, -1]
    slots = ids.shape[1]

    def mine(a):
        return lax.dynamic_slice_in_dim(a, first, groups, 0)

    ids_sent = lax.all_to_all(small_ids.T[:, None], PLANE, 0, 0, tiled=True)
    sizes = lax.dynamic_slice_in_dim(batch_sizes, me, 1, 1)[:, 0]

    pooled = pool(mine(ids), mine(used), mine(ends), table)
    arrived = lax.all_to_all(pooled, OWNERS, 0, 0, tiled=True)
    hot = (small_ids.T[:, :, None] == jnp.arange(small_rows, dtype=jnp.int32)).astype(BF16)
    small = jnp.einsum("tbr,tre->tbe", hot, small_tables, preferred_element_type=F32).astype(BF16)

    small_grad, folded = top(
        sizes, arrived, small, dense, labels[:, None], w_first, b_first[None], w_out[None], copies
    )

    grads = lax.all_to_all(small_grad, PLANE, 0, 0, tiled=True).reshape(-1, LANES)
    owner_hot = (ids_sent.reshape(-1)[:, None] == jnp.arange(small_rows, dtype=jnp.int32)).astype(BF16)
    partial = jnp.einsum("sr,se->re", owner_hot, grads, preferred_element_type=F32)
    total = lax.all_gather(partial, "x").sum(0)
    table_index = lax.axis_index(PLANE)
    mine_small = lax.dynamic_slice_in_dim(small_tables, table_index, 1, 0)[0]
    new_small = (mine_small.astype(F32) - step_size * total).astype(BF16)
    small_new = lax.all_gather(new_small, PLANE)

    folds = lax.all_to_all(folded.reshape((-1,) + folded.shape[2:]), ALL, 0, 0, tiled=True)
    large_new = scatter(ids, used, ends, folds, table)
    return small_new, large_new[None]


def solution(mesh):
    fine = Mesh(mesh.devices.reshape(2, 4, 2, 4, 2), ALL)
    placed = (
        P(ALL, None), P(ALL, None), P(ALL), P(), P(OWNERS, None, None), P(),
        P(OWNERS, None, None), P(OWNERS, None, None), P(), P(), P(),
    )
    return jax.shard_map(
        shards, mesh=fine, in_specs=placed, out_specs=(P(), P(OWNERS, None, None)), check_vma=False
    )
```

time: 932 us -> 362 us (0.39)
  local copies, waits for them, and re-layouts: 567 us -> 12 us
  Pallas kernels: 0 us -> 148 us
  other arithmetic: 130 us -> 2.9 us
  blocking collectives: 0 us -> 101 us
  waiting for transfers between devices: 124 us -> 47.3 us
  matrix products: 68.6 us -> 13.2 us
    gather x2 -> x0, local copies, waits for them, and re-layouts: 266 us -> none  [take_rows(): return table_one[row_list]]
    slice x194 -> x1, local copies, waits for them, and re-layouts: 192 us -> 1.61 us  [shards(): used = ends[:, -1]]
    pallas_call x0 -> x3, Pallas kernels: none -> 148 us  [the longest x1 64.1 us: scatter(): pl.pallas_call(functools.partial(scatter_kernel, group=group, unroll=16),...]
    all_to_all x0 -> x2, blocking collectives: none -> 101 us  [the longest x1 64.7 us: shards(): lax.all_to_all(folded.reshape((-1,) + folded.shape[2:]), ALL, 0, 0, tiled...]
    unnamed x8 -> x0, other arithmetic: 91.3 us -> none
    psum x1 -> x0, waiting for transfers between devices: 74.9 us -> none  [shards(): small_sum = lax.psum(small_local, ('rep', 'shard'))]
    unnamed x137 -> x9, local copies, waits for them, and re-layouts: 63 us -> 4.68 us
    dot_general x10 -> x2, matrix products: 68.6 us -> 13.2 us  [the longest x1 7.1 us: shards(): jnp.einsum('sr,se->re', owner_hot, grads, preferred_element_type=F32)]
  transfers between devices with their start and end apart: 4 -> 4, of which waited for: 3 -> 2; matrix products, arithmetic and copies ran while one was open for 14% -> 2% of each run, Pallas kernels for 0% -> 32%
where the time goes in v1:
time: 362 us; the launch traced here: 356 us
  Pallas kernels  148 us (41%)
  blocking collectives  101 us (28%)
  waiting for transfers between devices  47.3 us (13%)
  starting transfers between devices  17.9 us (5%)
  between operations  14.1 us (4%)
  matrix products  13.2 us (4%)
  local copies, waits for them, and re-layouts  12 us (3%)
    all_to_all x1, blocking collectives, shards(): lax.all_to_all(folded.reshape((-1,) + folded.shape[2:]), ALL, 0, 0, tiled...  64.7 us
    pallas_call x1, Pallas kernels, scatter(): pl.pallas_call(functools.partial(scatter_kernel, group=group, unroll=16),...  64.1 us
    pallas_call x1, Pallas kernels, top(): pl.pallas_call(functools.partial(top_kernel, pitch=pitch, vec_count=vec_c...  50.1 us
    all_to_all x1, blocking collectives, shards(): lax.all_to_all(small_grad, PLANE, 0, 0, tiled=True).reshape(-1, LANES)  36.5 us
    pallas_call x1, Pallas kernels, pool(): pl.pallas_call(functools.partial(pool_kernel, group=group, unroll=16), ou...  33.6 us
    all_to_all x1, waiting for transfers between devices, shards(): arrived = lax.all_to_all(pooled, OWNERS, 0, 0, tiled=True)  28.7 us
    all_gather x1, waiting for transfers between devices, shards(): total = lax.all_gather(partial, 'x').sum(0)  18.6 us
    all_to_all x1, starting transfers between devices, shards(): arrived = lax.all_to_all(pooled, OWNERS, 0, 0, tiled=True)  11.2 us
  transfers between devices with their start and end apart: 4, of which 2 were waited for; matrix products, arithmetic and copies ran while one was open for 2% of the time, Pallas kernels for 32%

profile of v1, /device:TPU:1, one launch (start us, length us, event | category | flops | bytes accessed | tf_op | source)
XLA Modules:
  0.0 356.4 jit_solution(13040753837223457046)
XLA Ops:
  7.2 0.0 copy-start
  7.2 1.4 dynamic-slice_bitcast_fusion.1.ends
  8.6 1.5 dynamic-slice_bitcast_fusion.ids
  10.0 1.6 slice_reduce_fusion
  11.6 0.7 dynamic-slice_reduce_fusion.used
  12.3 33.6 %pool.1 = bf16[64,128,128]{2,1,0:T(8,128)(2,1)} custom-call(s32[64,256]{1,0:T(8,128)} %dynamic-slice_bitcast_fusion.ids, s32[64]{0:T(128)} %dynamic-slice_reduce_fusion.used, s32[64,128]{1,0:T(8,128)} %dynamic-slice_bitcast_fusion.1.ends, bf16[8192,128]{1,0:T(8,128)(2,1)} %bitcast.22), custom_call_target="tpu_custom_call" | custom-call | tf_op jit(solution)/shard_map/pool/pallas_call | solution.py:71
  45.9 0.0 copy-start.2
  45.9 11.2 %all-to-all-start.1 = ((bf16[64,128,128]{2,1,0:T(8,128)(2,1)}), bf16[64,128,128]{2,1,0:T(8,128)(2,1)S(1)}, u32[]{:S(2)}, u32[]{:S(2)}) async-start(bf16[64,128,128]{2,1,0:T(8,128)(2,1)} %pool.1), calls=%async_computation.1 | async-start | bytes 4194304 | tf_op jit(solution)/shard_map/all_to_all | solution.py:371
  57.1 0.0 copy-done.2
  57.1 0.6 broadcast_in_dim.18
  57.8 28.7 %all-to-all-done.1.arrived = bf16[64,128,128]{2,1,0:T(8,128)(2,1)S(1)} async-done(((bf16[64,128,128]{2,1,0:T(8,128)(2,1)}), bf16[64,128,128]{2,1,0:T(8,128)(2,1)S(1)}, u32[]{:S(2)}, u32[]{:S(2)}) %all-to-all-start.1) | async-done | bytes 2097184 | tf_op jit(solution)/shard_map/all_to_all | solution.py:371
  86.5 0.0 copy-start.1
  86.5 6.4 %all-to-all-start = ((s32[32,1,256]{2,1,0:T(1,128)}), s32[32,1,256]{2,1,0:T(1,128)}, u32[]{:S(2)}, u32[]{:S(2)}) async-start(s32[32,1,256]{2,1,0:T(1,128)} %broadcast_in_dim.18), calls=%async_computation | async-start | bytes 65536 | tf_op jit(solution)/shard_map/all_to_all | solution.py:367
  92.9 0.0 copy-start.3
  92.9 0.2 all-gather.6.cloned.1.call-start
  93.1 6.1 %fusion.4.small = bf16[32,256,128]{2,1,0:T(8,128)(2,1)} fusion(bf16[32,512,128]{2,1,0:T(8,128)(2,1)} %param.14, s32[32,256]{1,0:T(8,128)S(1)} %bitcast.32), kind=kOutput, calls=%fused_computation.6 | convolution fusion | flops 1078984704 | bytes 6324224 | tf_op jit(solution)/shard_map/tbr,tre->tbe/dot_general | solution.py:373
  99.2 0.0 copy-done.1
  99.2 0.0 copy-done.3
  99.2 0.8 copy.14.labels
  100.0 0.0 copy-done
  100.0 0.8 dynamic-slice_reduce_fusion.1.sizes
  100.8 50.1 %top.1 = (bf16[32,256,128]{2,1,0:T(8,128)(2,1)}, bf16[2,64,128,128]{3,2,1,0:T(8,128)(2,1)}) custom-call(s32[64]{0:T(128)} %dynamic-slice_reduce_fusion.1.sizes, bf16[64,128,128]{2,1,0:T(8,128)(2,1)} %copy-done.1, bf16[32,256,128]{2,1,0:T(8,128)(2,1)} %fusion.4.small, bf16[256,128]{1,0:T(8,128)(2,1)} %dense.1, s32[256,1]{1,0:T(8,128)} %copy.14.labels, ...), custom_call_target="tpu_custom_call" | custom-call | tf_op jit(solution)/shard_map/top/pallas_call | solution.py:326
  150.9 0.0 all-to-all-done
  150.9 36.5 %all_to_all.20 = bf16[32,256,128]{2,1,0:T(8,128)(2,1)S(1)} all-to-all(bf16[32,256,128]{2,1,0:T(8,128)(2,1)} %get-tuple-element.4), channel_id=1, replica_groups=mesh['rep'=2,'y'=4,'zl'=2,'x'=4,'core'=2] {'rep','y','zl','core'}, dimensions={0} | all-to-all | bytes 4194304 | tf_op jit(solution)/shard_map/all_to_all | solution.py:379
  187.4 7.1 %fusion.1 = f32[512,128]{1,0:T(8,128)} fusion(bf16[8192,128]{1,0:T(8,128)(2,1)S(1)} %bitcast.25, s32[8192]{0:T(1024)} %bitcast.1), kind=kOutput, calls=%fused_computation.3 | convolution fusion | flops 1077936128 | bytes 2392064 | tf_op jit(solution)/shard_map/sr,se->re/dot_general | solution.py:381
  194.5 0.0 all-gather.6.cloned.1.call-update
  194.5 0.0 all-gather.4.cloned.1.call-start
  194.6 18.6 %all-gather.6.cloned.1.call-done = f32[2048,128]{1,0:T(8,128)} async-done(((f32[512,128]{1,0:T(8,128)}), f32[2048,128]{1,0:T(8,128)}) %all-gather.6.cloned.1.call-update) | async-done | bytes 1048592 | tf_op jit(solution)/shard_map/all_gather | solution.py:382
  213.2 1.3 reduce_sum.9
  214.5 1.6 fusion.5
  216.1 0.0 all-gather.4.cloned.1.call-update
  216.1 64.7 %all_to_all.21.folds = bf16[128,128,128]{2,1,0:T(8,128)(2,1)} all-to-all(bf16[128,128,128]{2,1,0:T(8,128)(2,1)} %bitcast.24), channel_id=1, replica_groups=mesh['rep'=2,'y'=4,'zl'=2,'x'=4,'core'=2] {'rep','y','zl','x','core'}, dimensions={0} | all-to-all | bytes 8388608 | tf_op jit(solution)/shard_map/all_to_all | solution.py:388
  280.9 64.1 %scatter.1 = bf16[8192,128]{1,0:T(8,128)(2,1)} custom-call(s32[128,256]{1,0:T(8,128)} %bitcast.30, s32[128]{0:T(128)} %get-tuple-element.6.used, s32[128,128]{1,0:T(8,128)} %bitcast.29, bf16[128,128,128]{2,1,0:T(8,128)(2,1)} %all_to_all.21.folds, bf16[8192,128]{1,0:T(8,128)(2,1)} %bitcast.23), custom_call_target="tpu_custom_call" | custom-call | tf_op jit(solution)/shard_map/scatter/pallas_call | solution.py:138
  344.9 0.0 all-gather.4.cloned.1.call-done
  344.9 4.7 %copy.16 = bf16[32,512,128]{2,1,0:T(8,128)(2,1)} copy(bf16[32,512,128]{2,1,0:T(8,128)(2,1)} %all-gather.4.cloned.1.call-done) | data formatting | bytes 8388608
Async XLA Ops:
  7.2 92.9 %copy-start = (s32[64,128]{1,0:T(8,128)S(1)}, s32[64,128]{1,0:T(8,128)}, u32[]{:S(2)}) copy-start(s32[64,128]{1,0:T(8,128)} %param.16) | copy-start | bytes 98308
  45.9 11.2 %copy-start.2 = (s32[256,32]{0,1:T(8,128)S(1)}, s32[256,32]{0,1:T(8,128)}, u32[]{:S(2)}) copy-start(s32[256,32]{0,1:T(8,128)} %param.12) | copy-start | bytes 98308
  45.9 40.6 %all-to-all-start.1 = ((bf16[64,128,128]{2,1,0:T(8,128)(2,1)}), bf16[64,128,128]{2,1,0:T(8,128)(2,1)S(1)}, u32[]{:S(2)}, u32[]{:S(2)}) async-start(bf16[64,128,128]{2,1,0:T(8,128)(2,1)} %pool.1), calls=%async_computation.1 | async-start | bytes 4194304 | tf_op jit(solution)/shard_map/all_to_all | solution.py:371
  86.5 12.8 %copy-start.1 = (bf16[64,128,128]{2,1,0:T(8,128)(2,1)}, bf16[64,128,128]{2,1,0:T(8,128)(2,1)S(1)}, u32[]{:S(2)}) copy-start(bf16[64,128,128]{2,1,0:T(8,128)(2,1)S(1)} %all-to-all-done.1.arrived) | copy-start | bytes 6291460
  86.5 64.4 %all-to-all-start = ((s32[32,1,256]{2,1,0:T(1,128)}), s32[32,1,256]{2,1,0:T(1,128)}, u32[]{:S(2)}, u32[]{:S(2)}) async-start(s32[32,1,256]{2,1,0:T(1,128)} %broadcast_in_dim.18), calls=%async_computation | async-start | bytes 65536 | tf_op jit(solution)/shard_map/all_to_all | solution.py:367
  92.9 6.4 %copy-start.3 = (s32[256]{0:T(256)S(1)}, s32[256]{0:T(256)}, u32[]{:S(2)}) copy-start(s32[256]{0:T(256)} %param.13) | copy-start | bytes 3076
  92.9 120.3 %all-gather.6.cloned.1.call-start = ((), (), s32[]{:S(2)}) async-start(), calls=%async_computation.5 | async-start | bytes 1310720 | tf_op jit(solution)/shard_map/all_gather | solution.py:382
  194.5 150.4 %all-gather.4.cloned.1.call-start = ((), (), s32[]{:S(2)}) async-start(), calls=%async_computation.4 | async-start | bytes 4325376 | tf_op jit(solution)/shard_map/all_gather | solution.py:386
Sparse Core Ops, SparseCore 0:
  194.7 18.4 all-gather.5
  216.2 105.2 all-gather.3

commit v2 on v1

--- a/solution.py
+++ b/solution.py
@@ -30,28 +30,37 @@
     return jnp.where(inside, 1.0, 0.0).astype(BF16)
 
 
-def pool_kernel(ids, used, ends, table, out, wide, rows, *, group, unroll):
-    dests, bags = ends.shape
-    slots = ids.shape[1]
+def cost(micros):
+    return pl.CostEstimate(flops=0, bytes_accessed=int(micros * 3.0e6), transcendentals=0)
+
+
+def slot_base(d, k, slots):
+    return (((d >> 3) * (slots // 128) + (k >> 7)) << 10) + ((d & 7) << 7) + (k & 127)
+
+
+def pool_kernel(first, ids, flat_ends, ends, table, out, wide, rows, *, group, unroll, slots):
+    dests, bags, _ = out.shape
     wide[...] = table[...].astype(F32)
     rows[...] = jnp.zeros(rows.shape, F32)
 
     def one_group(g, _):
         def one_dest(i, _):
-            d = g * group + i
-            base = i * slots
+            d = first[0] + g * group + i
+            row = i * slots
 
             def chunk(c, _):
-                first = c * unroll
+                start = slot_base(d, c * unroll, slots)
+                place = row + c * unroll
                 for u in range(unroll):
-                    rows[pl.ds(base + first + u, 1), :] = wide[pl.ds(ids[d, first + u], 1), :]
+                    rows[pl.ds(place + u, 1), :] = wide[pl.ds(ids[start + u], 1), :]
                 return 0
 
-            lax.fori_loop(0, (used[d] + unroll - 1) // unroll, chunk, 0)
+            used = flat_ends[d * bags + bags - 1]
+            lax.fori_loop(0, (used + unroll - 1) >> (unroll.bit_length() - 1), chunk, 0)
             return 0
 
         lax.fori_loop(0, group, one_dest, 0)
-        limits = ends[pl.ds(pl.multiple_of(g * group, group), group), :]
+        limits = ends[pl.ds(pl.multiple_of(first[0] + g * group, group), group), :]
         for i in range(group):
             mask = bag_mask(limits[i : i + 1], slots)
             taken = rows[i * slots : (i + 1) * slots, :].astype(BF16)
@@ -64,27 +73,26 @@
     lax.fori_loop(0, dests // group, one_group, 0)
 
 
-def pool(ids, used, ends, table):
-    dests, bags = ends.shape
-    slots = ids.shape[1]
+def pool(first, ids, flat_ends, ends, table, dests, slots):
+    bags = ends.shape[1]
     group = 8
     return pl.pallas_call(
-        functools.partial(pool_kernel, group=group, unroll=16),
+        functools.partial(pool_kernel, group=group, unroll=32, slots=slots),
         out_shape=jax.ShapeDtypeStruct((dests, bags, LANES), BF16),
-        in_specs=[whole(pltpu.SMEM), whole(pltpu.SMEM), whole(), whole()],
+        in_specs=[whole(pltpu.SMEM)] * 3 + [whole()] * 2,
         out_specs=whole(),
         scratch_shapes=[
             pltpu.VMEM(table.shape, F32),
             pltpu.VMEM((group * slots, LANES), F32),
         ],
         compiler_params=pltpu.CompilerParams(vmem_limit_bytes=VMEM_CAP),
+        cost_estimate=cost(16),
         name="pool",
-    )(ids, used, ends, table)
-
-
-def scatter_kernel(ids, used, ends, folds, table, out, vals, *accs, group, unroll):
+    )(first, ids, flat_ends, ends, table)
+
+
+def scatter_kernel(ids, flat_ends, ends, folds, table, out, vals, *accs, group, unroll, slots):
     dests, bags = ends.shape
-    slots = ids.shape[1]
     ways = len(accs)
     for acc in accs:
         acc[...] = jnp.zeros(acc.shape, F32)
@@ -99,21 +107,23 @@
 
         def one_dest(i, _):
             d = g * group + i
-            base = i * slots
+            row = i * slots
 
             def chunk(c, _):
-                first = c * unroll
+                start = slot_base(d, c * unroll, slots)
+                place = row + c * unroll
                 for v in range(0, unroll, ways):
-                    spots = [ids[d, first + v + w] for w in range(ways)]
+                    spots = [ids[start + v + w] for w in range(ways)]
                     sums = [
-                        accs[w][pl.ds(spots[w], 1), :] + vals[pl.ds(base + first + v + w, 1), :]
+                        accs[w][pl.ds(spots[w], 1), :] + vals[pl.ds(place + v + w, 1), :]
                         for w in range(ways)
                     ]
                     for w in range(ways):
                         accs[w][pl.ds(spots[w], 1), :] = sums[w]
                 return 0
 
-            lax.fori_loop(0, (used[d] + unroll - 1) // unroll, chunk, 0)
+            used = flat_ends[d * bags + bags - 1]
+            lax.fori_loop(0, (used + unroll - 1) >> (unroll.bit_length() - 1), chunk, 0)
             return 0
 
         lax.fori_loop(0, group, one_dest, 0)
@@ -132,19 +142,19 @@
     lax.fori_loop(0, table.shape[0] // 128, finish, 0)
 
 
-def scatter(ids, used, ends, folds, table, ways=4):
-    slots = ids.shape[1]
+def scatter(ids, flat_ends, ends, folds, table, slots, ways=8):
     group = 8
     return pl.pallas_call(
-        functools.partial(scatter_kernel, group=group, unroll=16),
+        functools.partial(scatter_kernel, group=group, unroll=32, slots=slots),
         out_shape=jax.ShapeDtypeStruct(table.shape, BF16),
-        in_specs=[whole(pltpu.SMEM), whole(pltpu.SMEM), whole(), whole(), whole()],
+        in_specs=[whole(pltpu.SMEM)] * 2 + [whole()] * 3,
         out_specs=whole(),
         scratch_shapes=[pltpu.VMEM((group * slots, LANES), F32)]
         + [pltpu.VMEM(table.shape, F32)] * ways,
         compiler_params=pltpu.CompilerParams(vmem_limit_bytes=VMEM_CAP),
+        cost_estimate=cost(28),
         name="scatter",
-    )(ids, used, ends, folds, table)
+    )(ids, flat_ends, ends, folds, table)
 
 
 def top_kernel(
@@ -340,11 +350,12 @@
             pltpu.VMEM((batch, up(pairs)), F32),
         ],
         compiler_params=pltpu.CompilerParams(vmem_limit_bytes=VMEM_CAP),
+        cost_estimate=cost(45),
         name="top",
     )(sizes, arrived, small, dense, labels, w_first, b_first, w_out)
 
 
-def shards(
+def step(
     dense, small_ids, labels, small_tables, large_tables,
     batch_sizes, bag_ends, owner_row_index, w_first, b_first, w_out,
 ):
@@ -354,20 +365,18 @@
     copies = lax.axis_size("rep")
     replica = lax.axis_index("rep")
     me = lax.axis_index(ALL)
-    first = replica * groups
     small_rows = small_tables.shape[1]
     table = large_tables[0]
-    ends, ids = bag_ends[0], owner_row_index[0]
-    used = ends[:, -1]
-    slots = ids.shape[1]
-
-    def mine(a):
-        return lax.dynamic_slice_in_dim(a, first, groups, 0)
+    ends = bag_ends[0]
+    slots = owner_row_index.shape[2]
+    flat_ends = ends.reshape(-1)
+    ids = owner_row_index.reshape(-1, 8, slots // 128, 128).transpose(0, 2, 1, 3).reshape(-1)
+    first = (replica * groups).astype(jnp.int32).reshape(1)
 
     ids_sent = lax.all_to_all(small_ids.T[:, None], PLANE, 0, 0, tiled=True)
     sizes = lax.dynamic_slice_in_dim(batch_sizes, me, 1, 1)[:, 0]
 
-    pooled = pool(mine(ids), mine(used), mine(ends), table)
+    pooled = pool(first, ids, flat_ends, ends, table, groups, slots)
     arrived = lax.all_to_all(pooled, OWNERS, 0, 0, tiled=True)
     hot = (small_ids.T[:, :, None] == jnp.arange(small_rows, dtype=jnp.int32)).astype(BF16)
     small = jnp.einsum("tbr,tre->tbe", hot, small_tables, preferred_element_type=F32).astype(BF16)
@@ -386,7 +395,7 @@
     small_new = lax.all_gather(new_small, PLANE)
 
     folds = lax.all_to_all(folded.reshape((-1,) + folded.shape[2:]), ALL, 0, 0, tiled=True)
-    large_new = scatter(ids, used, ends, folds, table)
+    large_new = scatter(ids, flat_ends, ends, folds, table, slots)
     return small_new, large_new[None]
 
 
@@ -397,5 +406,5 @@
         P(OWNERS, None, None), P(OWNERS, None, None), P(), P(), P(),
     )
     return jax.shard_map(
-        shards, mesh=fine, in_specs=placed, out_specs=(P(), P(OWNERS, None, None)), check_vma=False
+        step, mesh=fine, in_specs=placed, out_specs=(P(), P(OWNERS, None, None)), check_vma=False
     )

time: 362 us -> 315 us (0.87); the launches traced: 356 us -> 314 us
  Pallas kernels: 148 us -> 107 us
  local copies, waits for them, and re-layouts: 12 us -> 6.85 us
  waiting for transfers between devices: 47.3 us -> 51.1 us
    pallas_call x2, Pallas kernels: 97.6 us -> 56.9 us  [the longest x1 36.8 us: scatter(): pl.pallas_call(functools.partial(scatter_kernel, group=group, unroll=32,...]
    all_gather x2, waiting for transfers between devices: 18.6 us -> 22.4 us  [the longest x1 18.6 us: step(): total = lax.all_gather(partial, 'x').sum(0)]
  transfers between devices with their start and end apart: 4 -> 4, of which waited for: 2 -> 3; matrix products, arithmetic and copies ran while one was open for 2% -> 3% of each run, Pallas kernels for 32% -> 28%
where the time goes in v2:
time: 315 us; the launch traced here: 314 us
  Pallas kernels  107 us (34%)
  blocking collectives  101 us (32%)
  waiting for transfers between devices  51.1 us (16%)
  starting transfers between devices  17.4 us (6%)
  between operations  14.1 us (4%)
  matrix products  13.2 us (4%)
  local copies, waits for them, and re-layouts  6.85 us (2%)
    all_to_all x1, blocking collectives, step(): lax.all_to_all(folded.reshape((-1,) + folded.shape[2:]), ALL, 0, 0, tiled...  64.7 us
    pallas_call x1, Pallas kernels, top(): pl.pallas_call(functools.partial(top_kernel, pitch=pitch, vec_count=vec_c...  50.1 us
    pallas_call x1, Pallas kernels, scatter(): pl.pallas_call(functools.partial(scatter_kernel, group=group, unroll=32,...  36.8 us
    all_to_all x1, blocking collectives, step(): lax.all_to_all(small_grad, PLANE, 0, 0, tiled=True).reshape(-1, LANES)  36.5 us
    all_to_all x1, waiting for transfers between devices, step(): arrived = lax.all_to_all(pooled, OWNERS, 0, 0, tiled=True)  28.7 us
    pallas_call x1, Pallas kernels, pool(): pl.pallas_call(functools.partial(pool_kernel, group=group, unroll=32, slo...  20.1 us
    all_gather x1, waiting for transfers between devices, step(): total = lax.all_gather(partial, 'x').sum(0)  18.6 us
    all_to_all x1, starting transfers between devices, step(): arrived = lax.all_to_all(pooled, OWNERS, 0, 0, tiled=True)  11.1 us
  transfers between devices with their start and end apart: 4, of which 3 were waited for; matrix products, arithmetic and copies ran while one was open for 3% of the time, Pallas kernels for 28%

profile of v2, /device:TPU:1, one launch (start us, length us, event | category | flops | bytes accessed | tf_op | source)
XLA Modules:
  0.0 313.9 jit_solution(8200485789223520754)
XLA Ops:
  7.2 0.0 copy-start
  7.2 20.1 %pool.1 = bf16[64,128,128]{2,1,0:T(8,128)(2,1)} custom-call(s32[1]{0:T(128)} %bitcast.2.first, s32[32768]{0:T(1024)} %bitcast.34, s32[16384]{0:T(1024)} %bitcast.29, s32[128,128]{1,0:T(8,128)} %bitcast.30, bf16[8192,128]{1,0:T(8,128)(2,1)} %bitcast.24), custom_call_target="tpu_custom_call" | custom-call | bytes 48000000 | tf_op jit(solution)/shard_map/pool/pallas_call | solution.py:79
  27.3 0.0 copy-start.2
  27.3 11.1 %all-to-all-start.1 = ((bf16[64,128,128]{2,1,0:T(8,128)(2,1)}), bf16[64,128,128]{2,1,0:T(8,128)(2,1)S(1)}, u32[]{:S(2)}, u32[]{:S(2)}) async-start(bf16[64,128,128]{2,1,0:T(8,128)(2,1)} %pool.1), calls=%async_computation.1 | async-start | bytes 4194304 | tf_op jit(solution)/shard_map/all_to_all | solution.py:380
  38.4 0.0 copy-done.2
  38.4 0.6 broadcast_in_dim.18
  39.0 28.7 %all-to-all-done.1.arrived = bf16[64,128,128]{2,1,0:T(8,128)(2,1)S(1)} async-done(((bf16[64,128,128]{2,1,0:T(8,128)(2,1)}), bf16[64,128,128]{2,1,0:T(8,128)(2,1)S(1)}, u32[]{:S(2)}, u32[]{:S(2)}) %all-to-all-start.1) | async-done | bytes 2097184 | tf_op jit(solution)/shard_map/all_to_all | solution.py:380
  67.7 0.0 copy-start.1
  67.7 6.1 %all-to-all-start = ((s32[32,1,256]{2,1,0:T(1,128)}), s32[32,1,256]{2,1,0:T(1,128)}, u32[]{:S(2)}, u32[]{:S(2)}) async-start(s32[32,1,256]{2,1,0:T(1,128)} %broadcast_in_dim.18), calls=%async_computation | async-start | bytes 65536 | tf_op jit(solution)/shard_map/all_to_all | solution.py:376
  73.8 0.0 copy-start.3
  73.8 0.2 all-gather.6.cloned.1.call-start
  74.0 6.1 %fusion.4.small = bf16[32,256,128]{2,1,0:T(8,128)(2,1)} fusion(bf16[32,512,128]{2,1,0:T(8,128)(2,1)} %param.14, s32[32,256]{1,0:T(8,128)S(1)} %bitcast.37), kind=kOutput, calls=%fused_computation.6 | convolution fusion | flops 1078984704 | bytes 6324224 | tf_op jit(solution)/shard_map/tbr,tre->tbe/dot_general | solution.py:382
  80.1 0.0 copy-done.1
  80.2 0.0 copy-done.3
  80.2 0.8 copy.14.labels
  80.9 0.0 copy-done
  80.9 0.8 dynamic-slice_reduce_fusion.sizes
  81.7 50.1 %top.1 = (bf16[32,256,128]{2,1,0:T(8,128)(2,1)}, bf16[2,64,128,128]{3,2,1,0:T(8,128)(2,1)}) custom-call(s32[64]{0:T(128)} %dynamic-slice_reduce_fusion.sizes, bf16[64,128,128]{2,1,0:T(8,128)(2,1)} %copy-done.1, bf16[32,256,128]{2,1,0:T(8,128)(2,1)} %fusion.4.small, bf16[256,128]{1,0:T(8,128)(2,1)} %dense.1, s32[256,1]{1,0:T(8,128)} %copy.14.labels, ...), custom_call_target="tpu_custom_call" | custom-call | bytes 135000000 | tf_op jit(solution)/shard_map/top/pallas_call | solution.py:336
  131.8 0.0 all-to-all-done
  131.8 36.5 %all_to_all.20 = bf16[32,256,128]{2,1,0:T(8,128)(2,1)S(1)} all-to-all(bf16[32,256,128]{2,1,0:T(8,128)(2,1)} %get-tuple-element.4), channel_id=1, replica_groups=mesh['rep'=2,'y'=4,'zl'=2,'x'=4,'core'=2] {'rep','y','zl','core'}, dimensions={0} | all-to-all | bytes 4194304 | tf_op jit(solution)/shard_map/all_to_all | solution.py:388
  168.3 7.1 %fusion.1 = f32[512,128]{1,0:T(8,128)} fusion(bf16[8192,128]{1,0:T(8,128)(2,1)S(1)} %bitcast.27, s32[8192]{0:T(1024)} %bitcast.1), kind=kOutput, calls=%fused_computation.3 | convolution fusion | flops 1077936128 | bytes 2392064 | tf_op jit(solution)/shard_map/sr,se->re/dot_general | solution.py:390
  175.4 0.0 all-gather.6.cloned.1.call-update
  175.4 0.0 all-gather.4.cloned.1.call-start
  175.5 18.6 %all-gather.6.cloned.1.call-done = f32[2048,128]{1,0:T(8,128)} async-done(((f32[512,128]{1,0:T(8,128)}), f32[2048,128]{1,0:T(8,128)}) %all-gather.6.cloned.1.call-update) | async-done | bytes 1048592 | tf_op jit(solution)/shard_map/all_gather | solution.py:391
  194.1 1.3 reduce_sum.9
  195.4 1.6 fusion.5
  197.0 0.0 all-gather.4.cloned.1.call-update
  197.1 64.7 %all_to_all.21.folds = bf16[128,128,128]{2,1,0:T(8,128)(2,1)} all-to-all(bf16[128,128,128]{2,1,0:T(8,128)(2,1)} %bitcast.26), channel_id=1, replica_groups=mesh['rep'=2,'y'=4,'zl'=2,'x'=4,'core'=2] {'rep','y','zl','x','core'}, dimensions={0} | all-to-all | bytes 8388608 | tf_op jit(solution)/shard_map/all_to_all | solution.py:397
  261.8 36.8 %scatter.1 = bf16[8192,128]{1,0:T(8,128)(2,1)} custom-call(s32[32768]{0:T(1024)} %bitcast.35, s32[16384]{0:T(1024)} %bitcast.31, s32[128,128]{1,0:T(8,128)} %bitcast.32, bf16[128,128,128]{2,1,0:T(8,128)(2,1)} %all_to_all.21.folds, bf16[8192,128]{1,0:T(8,128)(2,1)} %bitcast.25), custom_call_target="tpu_custom_call" | custom-call | bytes 84000000 | tf_op jit(solution)/shard_map/scatter/pallas_call | solution.py:147
  298.6 3.8 %all-gather.4.cloned.1.call-done = bf16[32,512,128]{2,1,0:T(8,128)(2,1)} async-done(((bf16[1,512,128]{2,1,0:T(8,128)(2,1)}), bf16[32,512,128]{2,1,0:T(8,128)(2,1)}) %all-gather.4.cloned.1.call-update) | async-done | bytes 4194320 | tf_op jit(solution)/shard_map/all_gather | solution.py:395
  302.4 4.7 %copy.16 = bf16[32,512,128]{2,1,0:T(8,128)(2,1)} copy(bf16[32,512,128]{2,1,0:T(8,128)(2,1)} %all-gather.4.cloned.1.call-done) | data formatting | bytes 8388608
Async XLA Ops:
  7.2 73.8 %copy-start = (s32[64,128]{1,0:T(8,128)S(1)}, s32[64,128]{1,0:T(8,128)}, u32[]{:S(2)}) copy-start(s32[64,128]{1,0:T(8,128)} %param.16) | copy-start | bytes 98308
  27.3 11.1 %copy-start.2 = (s32[256,32]{0,1:T(8,128)S(1)}, s32[256,32]{0,1:T(8,128)}, u32[]{:S(2)}) copy-start(s32[256,32]{0,1:T(8,128)} %param.12) | copy-start | bytes 98308
  27.3 40.4 %all-to-all-start.1 = ((bf16[64,128,128]{2,1,0:T(8,128)(2,1)}), bf16[64,128,128]{2,1,0:T(8,128)(2,1)S(1)}, u32[]{:S(2)}, u32[]{:S(2)}) async-start(bf16[64,128,128]{2,1,0:T(8,128)(2,1)} %pool.1), calls=%async_computation.1 | async-start | bytes 4194304 | tf_op jit(solution)/shard_map/all_to_all | solution.py:380
  67.7 12.5 %copy-start.1 = (bf16[64,128,128]{2,1,0:T(8,128)(2,1)}, bf16[64,128,128]{2,1,0:T(8,128)(2,1)S(1)}, u32[]{:S(2)}) copy-start(bf16[64,128,128]{2,1,0:T(8,128)(2,1)S(1)} %all-to-all-done.1.arrived) | copy-start | bytes 6291460
  67.7 64.1 %all-to-all-start = ((s32[32,1,256]{2,1,0:T(1,128)}), s32[32,1,256]{2,1,0:T(1,128)}, u32[]{:S(2)}, u32[]{:S(2)}) async-start(s32[32,1,256]{2,1,0:T(1,128)} %broadcast_in_dim.18), calls=%async_computation | async-start | bytes 65536 | tf_op jit(solution)/shard_map/all_to_all | solution.py:376
  73.8 6.4 %copy-start.3 = (s32[256]{0:T(256)S(1)}, s32[256]{0:T(256)}, u32[]{:S(2)}) copy-start(s32[256]{0:T(256)} %param.13) | copy-start | bytes 3076
  73.8 120.3 %all-gather.6.cloned.1.call-start = ((), (), s32[]{:S(2)}) async-start(), calls=%async_computation.5 | async-start | bytes 1310720 | tf_op jit(solution)/shard_map/all_gather | solution.py:391
  175.4 127.0 %all-gather.4.cloned.1.call-start = ((), (), s32[]{:S(2)}) async-start(), calls=%async_computation.4 | async-start | bytes 4325376 | tf_op jit(solution)/shard_map/all_gather | solution.py:395
Sparse Core Ops, SparseCore 0:
  175.6 18.4 all-gather.5
  197.2 105.2 all-gather.3

commit v3 on v2

--- a/solution.py
+++ b/solution.py
@@ -8,6 +8,7 @@
 
 step_size = 32.0
 LANES = 128
+WAYS = 8
 VMEM_CAP = 67_000_000
 F32 = jnp.float32
 BF16 = jnp.bfloat16
@@ -21,15 +22,27 @@
     return pl.BlockSpec(memory_space=space)
 
 
-def bag_mask(ends_row, slots):
+def bag_mask(ends_row, slots, part, parts):
     bags = ends_row.shape[1]
+    size = bags // parts
     lane = lax.broadcasted_iota(jnp.int32, (1, bags), 1)
     starts = jnp.where(lane == 0, 0, pltpu.roll(ends_row, 1, 1))
-    slot = lax.broadcasted_iota(jnp.int32, (slots, bags), 0)
+    if part:
+        starts = pltpu.roll(starts, bags - part * size, 1)
+        ends_row = pltpu.roll(ends_row, bags - part * size, 1)
+    starts, ends_row = starts[:, :size], ends_row[:, :size]
+    slot = lax.broadcasted_iota(jnp.int32, (slots, size), 0)
     inside = (slot >= starts) & (slot < ends_row)
     return jnp.where(inside, 1.0, 0.0).astype(BF16)
 
 
+def slot_span(flat_ends, d, bags, part, parts, unroll):
+    size = bags // parts
+    step = unroll.bit_length() - 1
+    low = flat_ends[d * bags + part * size - 1] >> step if part else 0
+    return low, (flat_ends[d * bags + (part + 1) * size - 1] + unroll - 1) >> step
+
+
 def cost(micros):
     return pl.CostEstimate(flops=0, bytes_accessed=int(micros * 3.0e6), transcendentals=0)
 
@@ -38,9 +51,16 @@
     return (((d >> 3) * (slots // 128) + (k >> 7)) << 10) + ((d & 7) << 7) + (k & 127)
 
 
-def pool_kernel(first, ids, flat_ends, ends, table, out, wide, rows, *, group, unroll, slots):
-    dests, bags, _ = out.shape
-    wide[...] = table[...].astype(F32)
+def pool_kernel(first, ids, flat_ends, ends, table, out, wide, rows, *, group, unroll, slots, part, parts):
+    dests = out.shape[0]
+    bags = ends.shape[1]
+
+    def widen(c, _):
+        span = pl.ds(pl.multiple_of(c * 256, 256), 256)
+        wide[span, :] = table[span, :].astype(F32)
+        return 0
+
+    lax.fori_loop(0, table.shape[0] // 256, widen, 0)
     rows[...] = jnp.zeros(rows.shape, F32)
 
     def one_group(g, _):
@@ -55,14 +75,14 @@
                     rows[pl.ds(place + u, 1), :] = wide[pl.ds(ids[start + u], 1), :]
                 return 0
 
-            used = flat_ends[d * bags + bags - 1]
-            lax.fori_loop(0, (used + unroll - 1) >> (unroll.bit_length() - 1), chunk, 0)
+            low, high = slot_span(flat_ends, d, bags, part, parts, unroll)
+            lax.fori_loop(low, high, chunk, 0)
             return 0
 
         lax.fori_loop(0, group, one_dest, 0)
         limits = ends[pl.ds(pl.multiple_of(first[0] + g * group, group), group), :]
         for i in range(group):
-            mask = bag_mask(limits[i : i + 1], slots)
+            mask = bag_mask(limits[i : i + 1], slots, part, parts)
             taken = rows[i * slots : (i + 1) * slots, :].astype(BF16)
             total = lax.dot_general(
                 mask, taken, (((0,), (0,)), ((), ())), preferred_element_type=F32
@@ -73,12 +93,14 @@
     lax.fori_loop(0, dests // group, one_group, 0)
 
 
-def pool(first, ids, flat_ends, ends, table, dests, slots):
+def pool(first, ids, flat_ends, ends, table, dests, slots, part, parts):
     bags = ends.shape[1]
     group = 8
     return pl.pallas_call(
-        functools.partial(pool_kernel, group=group, unroll=32, slots=slots),
-        out_shape=jax.ShapeDtypeStruct((dests, bags, LANES), BF16),
+        functools.partial(
+            pool_kernel, group=group, unroll=32, slots=slots, part=part, parts=parts
+        ),
+        out_shape=jax.ShapeDtypeStruct((dests, bags // parts, LANES), BF16),
         in_specs=[whole(pltpu.SMEM)] * 3 + [whole()] * 2,
         out_specs=whole(),
         scratch_shapes=[
@@ -86,21 +108,27 @@
             pltpu.VMEM((group * slots, LANES), F32),
         ],
         compiler_params=pltpu.CompilerParams(vmem_limit_bytes=VMEM_CAP),
-        cost_estimate=cost(16),
+        cost_estimate=cost(12),
         name="pool",
     )(first, ids, flat_ends, ends, table)
 
 
-def scatter_kernel(ids, flat_ends, ends, folds, table, out, vals, *accs, group, unroll, slots):
+def scatter_kernel(ids, flat_ends, ends, folds, *rest, group, unroll, slots, part, parts, ways):
+    before, table, out = (None, None) + rest[:1] if part == 0 else rest[:3]
+    vals, *accs = rest[1 if part == 0 else 3 :]
     dests, bags = ends.shape
-    ways = len(accs)
-    for acc in accs:
-        acc[...] = jnp.zeros(acc.shape, F32)
+
+    def clear(c, _):
+        for acc in accs:
+            acc[pl.ds(pl.multiple_of(c * 128, 128), 128), :] = jnp.zeros((128, LANES), F32)
+        return 0
+
+    lax.fori_loop(0, out.shape[0] // 128, clear, 0)
 
     def one_group(g, _):
         limits = ends[pl.ds(pl.multiple_of(g * group, group), group), :]
         for i in range(group):
-            mask = bag_mask(limits[i : i + 1], slots)
+            mask = bag_mask(limits[i : i + 1], slots, part, parts)
             vals[i * slots : (i + 1) * slots, :] = jnp.dot(
                 mask, folds[g * group + i], preferred_element_type=F32
             )
@@ -122,8 +150,8 @@
                         accs[w][pl.ds(spots[w], 1), :] = sums[w]
                 return 0
 
-            used = flat_ends[d * bags + bags - 1]
-            lax.fori_loop(0, (used + unroll - 1) >> (unroll.bit_length() - 1), chunk, 0)
+            low, high = slot_span(flat_ends, d, bags, part, parts, unroll)
+            lax.fori_loop(low, high, chunk, 0)
             return 0
 
         lax.fori_loop(0, group, one_dest, 0)
@@ -136,34 +164,46 @@
         total = accs[0][span, :]
         for acc in accs[1:]:
             total = total + acc[span, :]
-        out[span, :] = (table[span, :].astype(F32) - step_size * total).astype(BF16)
-        return 0
-
-    lax.fori_loop(0, table.shape[0] // 128, finish, 0)
-
-
-def scatter(ids, flat_ends, ends, folds, table, slots, ways=8):
+        if part:
+            total = total + before[span, :]
+        if part < parts - 1:
+            out[span, :] = total
+        else:
+            out[span, :] = (table[span, :].astype(F32) - step_size * total).astype(BF16)
+        return 0
+
+    lax.fori_loop(0, out.shape[0] // 128, finish, 0)
+
+
+def scatter(ids, flat_ends, ends, folds, before, table, slots, part, parts, ways):
     group = 8
+    last = part == parts - 1
+    extra = () if part == 0 else (before, table)
     return pl.pallas_call(
-        functools.partial(scatter_kernel, group=group, unroll=32, slots=slots),
-        out_shape=jax.ShapeDtypeStruct(table.shape, BF16),
-        in_specs=[whole(pltpu.SMEM)] * 2 + [whole()] * 3,
+        functools.partial(
+            scatter_kernel, group=group, unroll=32, slots=slots, part=part, parts=parts, ways=ways
+        ),
+        out_shape=jax.ShapeDtypeStruct(table.shape, BF16 if last else F32),
+        in_specs=[whole(pltpu.SMEM)] * 2 + [whole()] * (2 + len(extra)),
         out_specs=whole(),
         scratch_shapes=[pltpu.VMEM((group * slots, LANES), F32)]
         + [pltpu.VMEM(table.shape, F32)] * ways,
         compiler_params=pltpu.CompilerParams(vmem_limit_bytes=VMEM_CAP),
-        cost_estimate=cost(28),
+        cost_estimate=cost(14 if last else 26),
         name="scatter",
-    )(ids, flat_ends, ends, folds, table)
+    )(ids, flat_ends, ends, folds, *extra)
 
 
 def top_kernel(
-    sizes, arrived, small, dense, labels, w_first, b_first, w_out,
-    small_out, fold_out,
-    vec, gram, feats, preact, pre_grad, pair_grad,
+    sizes, arrived_low, arrived_high, small, dense, labels, w_far, b_first, w_out,
+    small_out, fold_low, fold_high,
+    vec, gram, feats, preact, pre_grad, pair_grad, w_first, w_sem,
     *, pitch, vec_count,
 ):
-    feat_count, bags, width = arrived.shape
+    weights = pltpu.make_async_copy(w_far, w_first, w_sem)
+    weights.start()
+    feat_count, half, width = arrived_low.shape
+    bags = 2 * half
     small_count, batch, _ = small.shape
     shift = batch.bit_length() - 1
     pairs = vec_count * (vec_count - 1) // 2
@@ -184,7 +224,9 @@
     bag = lax.broadcasted_iota(jnp.int32, (batch, bags), 1)
     for f in range(feat_count):
         hot = jnp.where(((sample * sizes[f]) >> shift) == bag, 1.0, 0.0).astype(BF16)
-        vec[column(first_large + f), :] = jnp.dot(hot, arrived[f], preferred_element_type=F32)
+        vec[column(first_large + f), :] = jnp.dot(
+            hot, jnp.concatenate([arrived_low[f], arrived_high[f]], axis=0), preferred_element_type=F32
+        )
 
     together = 8
 
@@ -235,6 +277,7 @@
 
     lax.fori_loop(0, batch // part, pack_step, 0)
 
+    weights.wait()
     depth = pairs + width
     bulk = depth // LANES * LANES
     wide = 256
@@ -294,17 +337,14 @@
         found = []
         for n in range(together):
             spot = pl.multiple_of(base + n * pitch, 8)
-            lower = gram[pl.ds(spot, pitch), :].astype(BF16)
-            vectors = vec[pl.ds(spot, LANES), :].astype(BF16)
+            lower = gram[pl.ds(spot, pitch), :]
+            vectors = vec[pl.ds(spot, pitch), :].astype(BF16)
             found.append((lower, vectors))
         for n in range(together):
             lower, vectors = found[n]
             spot = pl.multiple_of(base + n * pitch, 8)
-            one = jnp.dot(lower, vectors, preferred_element_type=F32)
-            two = lax.dot_general(
-                lower, vectors[:pitch], (((0,), (0,)), ((), ())), preferred_element_type=F32
-            )
-            vec[pl.ds(spot, pitch), :] = one + two[:pitch]
+            both = (lower[:, :pitch] + jnp.transpose(lower)[:pitch, :]).astype(BF16)
+            vec[pl.ds(spot, pitch), :] = jnp.dot(both, vectors, preferred_element_type=F32)
         return 0
 
     lax.fori_loop(0, batch // together, grad_step, 0)
@@ -317,12 +357,13 @@
         hot = jnp.where(((sample_t * sizes[f]) >> shift) == bag_t, 1.0, 0.0).astype(BF16)
         grads = vec[column(first_large + f), :].astype(BF16)
         fold = jnp.dot(hot, grads, preferred_element_type=F32).astype(BF16)
-        for copy in range(fold_out.shape[0]):
-            fold_out[copy, f] = fold
+        for copy in range(fold_low.shape[0]):
+            fold_low[copy, f] = fold[:half]
+            fold_high[copy, f] = fold[half:]
 
 
 def top(sizes, arrived, small, dense, labels, w_first, b_first, w_out, copies):
-    feat_count, bags, width = arrived.shape
+    feat_count, half, width = arrived[0].shape
     small_count, batch, _ = small.shape
     vec_count = 1 + small_count + feat_count
     pitch = -(-vec_count // 8) * 8
@@ -337,10 +378,11 @@
         functools.partial(top_kernel, pitch=pitch, vec_count=vec_count),
         out_shape=(
             jax.ShapeDtypeStruct((small_count, batch, width), BF16),
-            jax.ShapeDtypeStruct((copies, feat_count, bags, width), BF16),
+            jax.ShapeDtypeStruct((copies, feat_count, half, width), BF16),
+            jax.ShapeDtypeStruct((copies, feat_count, half, width), BF16),
         ),
-        in_specs=[whole(pltpu.SMEM)] + [whole()] * 7,
-        out_specs=(whole(), whole()),
+        in_specs=[whole(pltpu.SMEM)] + [whole()] * 5 + [whole(pl.ANY)] + [whole()] * 2,
+        out_specs=(whole(),) * 3,
         scratch_shapes=[
             pltpu.VMEM((batch * pitch + LANES - pitch, width), F32),
             pltpu.VMEM((batch * pitch, LANES), F32),
@@ -348,11 +390,13 @@
             pltpu.VMEM((batch, hidden), F32),
             pltpu.VMEM((batch, hidden), BF16),
             pltpu.VMEM((batch, up(pairs)), F32),
+            pltpu.VMEM(w_first.shape, BF16),
+            pltpu.SemaphoreType.DMA,
         ],
         compiler_params=pltpu.CompilerParams(vmem_limit_bytes=VMEM_CAP),
         cost_estimate=cost(45),
         name="top",
-    )(sizes, arrived, small, dense, labels, w_first, b_first, w_out)
+    )(sizes, *arrived, small, dense, labels, w_first, b_first, w_out)
 
 
 def step(
@@ -376,26 +420,37 @@
     ids_sent = lax.all_to_all(small_ids.T[:, None], PLANE, 0, 0, tiled=True)
     sizes = lax.dynamic_slice_in_dim(batch_sizes, me, 1, 1)[:, 0]
 
-    pooled = pool(first, ids, flat_ends, ends, table, groups, slots)
-    arrived = lax.all_to_all(pooled, OWNERS, 0, 0, tiled=True)
+    parts = 2
+    arrived = []
+    for part in range(parts):
+        pooled = pool(first, ids, flat_ends, ends, table, groups, slots, part, parts)
+        arrived.append(lax.all_to_all(pooled, OWNERS, 0, 0, tiled=True))
     hot = (small_ids.T[:, :, None] == jnp.arange(small_rows, dtype=jnp.int32)).astype(BF16)
     small = jnp.einsum("tbr,tre->tbe", hot, small_tables, preferred_element_type=F32).astype(BF16)
 
-    small_grad, folded = top(
+    small_grad, *folded = top(
         sizes, arrived, small, dense, labels[:, None], w_first, b_first[None], w_out[None], copies
     )
 
     grads = lax.all_to_all(small_grad, PLANE, 0, 0, tiled=True).reshape(-1, LANES)
     owner_hot = (ids_sent.reshape(-1)[:, None] == jnp.arange(small_rows, dtype=jnp.int32)).astype(BF16)
     partial = jnp.einsum("sr,se->re", owner_hot, grads, preferred_element_type=F32)
-    total = lax.all_gather(partial, "x").sum(0)
+    found = lax.all_gather(partial.astype(BF16), "x")
+    total = found.astype(F32).sum(0)
     table_index = lax.axis_index(PLANE)
     mine_small = lax.dynamic_slice_in_dim(small_tables, table_index, 1, 0)[0]
     new_small = (mine_small.astype(F32) - step_size * total).astype(BF16)
-    small_new = lax.all_gather(new_small, PLANE)
-
-    folds = lax.all_to_all(folded.reshape((-1,) + folded.shape[2:]), ALL, 0, 0, tiled=True)
-    large_new = scatter(ids, flat_ends, ends, folds, table, slots)
+    chips = lax.all_gather(new_small, PLANE[:-1])
+    across = lax.ppermute(chips, "core", [(0, 1), (1, 0)])
+    shape = (chips.shape[0], 2) + chips.shape[1:]
+    here = lax.broadcasted_iota(jnp.int32, shape, 1) == lax.axis_index("core")
+    small_new = jnp.where(here, chips[:, None], across[:, None]).reshape(small_tables.shape)
+
+    large_new = None
+    for part in range(parts):
+        fold = folded[part].reshape((-1,) + folded[part].shape[2:])
+        folds = lax.all_to_all(fold, ALL, 0, 0, tiled=True)
+        large_new = scatter(ids, flat_ends, ends, folds, large_new, table, slots, part, parts, WAYS)
     return small_new, large_new[None]
 
 

time: 315 us -> 372 us (1.18)
  blocking collectives: 101 us -> 10.8 us
  waiting for transfers between devices: 51.1 us -> 130 us
  starting transfers between devices: 17.4 us -> 54.7 us
  Pallas kernels: 107 us -> 139 us
  local copies, waits for them, and re-layouts: 6.85 us -> 3.07 us
    all_to_all x2 -> x0, blocking collectives: 101 us -> none  [the longest x1 64.7 us: step(): lax.all_to_all(folded.reshape((-1,) + folded.shape[2:]), ALL, 0, 0, tiled...]
    all_gather x2 -> x1, waiting for transfers between devices: 22.4 us -> 79.3 us  [step(): chips = lax.all_gather(new_small, PLANE[:-1])]
    all_to_all x1 -> x5, starting transfers between devices: 11.1 us -> 39.5 us  [the longest x2 16.3 us: step(): arrived.append(lax.all_to_all(pooled, OWNERS, 0, 0, tiled=True))]
    pallas_call x1 -> x2, Pallas kernels: 36.8 us -> 61.1 us  [scatter(): pl.pallas_call(functools.partial(scatter_kernel, group=group, unroll=32,...]
    all_to_all x1 -> x5, waiting for transfers between devices: 28.7 us -> 50.7 us  [the longest x1 30.5 us: step(): lax.all_to_all(small_grad, PLANE, 0, 0, tiled=True).reshape(-1, LANES)]
    pallas_call x1 -> x2, Pallas kernels: 20.1 us -> 31.6 us  [pool(): pl.pallas_call(functools.partial(pool_kernel, group=group, unroll=32, slo...]
    all_gather x0 -> x1, blocking collectives: none -> 10.8 us  [step(): found = lax.all_gather(partial.astype(BF16), 'x')]
    ppermute x0 -> x1, starting transfers between devices: none -> 8.81 us  [step(): across = lax.ppermute(chips, 'core', [(0, 1), (1, 0)])]
  transfers between devices with their start and end apart: 4 -> 8, of which waited for: 3 -> 4; matrix products, arithmetic and copies ran while one was open for 3% -> 2% of each run, Pallas kernels for 28% -> 33%
where the time goes in v3:
time: 372 us; the launch traced here: 371 us
  Pallas kernels  139 us (37%)
  waiting for transfers between devices  130 us (35%)
  starting transfers between devices  54.7 us (15%)
  between operations  14.2 us (4%)
  matrix products  12.5 us (3%)
  blocking collectives  10.8 us (3%)
  other arithmetic  6.27 us (2%)
    all_gather x1, waiting for transfers between devices, step(): chips = lax.all_gather(new_small, PLANE[:-1])  79.3 us
    pallas_call x2, Pallas kernels, scatter(): pl.pallas_call(functools.partial(scatter_kernel, group=group, unroll=32,...  61.1 us
    pallas_call x1, Pallas kernels, top(): pl.pallas_call(functools.partial(top_kernel, pitch=pitch, vec_count=vec_c...  46.4 us
    pallas_call x2, Pallas kernels, pool(): pl.pallas_call(functools.partial(pool_kernel, group=group, unroll=32, slo...  31.6 us
    all_to_all x1, waiting for transfers between devices, step(): lax.all_to_all(small_grad, PLANE, 0, 0, tiled=True).reshape(-1, LANES)  30.5 us
    all_to_all x2, waiting for transfers between devices, step(): arrived.append(lax.all_to_all(pooled, OWNERS, 0, 0, tiled=True))  20.2 us
    all_to_all x2, starting transfers between devices, step(): arrived.append(lax.all_to_all(pooled, OWNERS, 0, 0, tiled=True))  16.3 us
    all_to_all x2, starting transfers between devices, step(): folds = lax.all_to_all(fold, ALL, 0, 0, tiled=True)  15.8 us
  transfers between devices with their start and end apart: 8, of which 4 were waited for; matrix products, arithmetic and copies ran while one was open for 2% of the time, Pallas kernels for 33%

profile of v3, /device:TPU:1, one launch (start us, length us, event | category | flops | bytes accessed | tf_op | source)
XLA Modules:
  0.0 370.7 jit_solution(8856348448142152737)
XLA Ops:
  7.2 0.0 copy-start
  7.2 17.2 %pool.2 = bf16[64,64,128]{2,1,0:T(8,128)(2,1)} custom-call(s32[1]{0:T(128)} %bitcast.2.first, s32[32768]{0:T(1024)} %bitcast.41, s32[16384]{0:T(1024)} %bitcast.33, s32[128,128]{1,0:T(8,128)} %bitcast.34, bf16[8192,128]{1,0:T(8,128)(2,1)} %bitcast.30), custom_call_target="tpu_custom_call" | custom-call | bytes 36000000 | tf_op jit(solution)/shard_map/pool/pallas_call | solution.py:99
  24.4 10.8 %all-to-all-start.1 = ((bf16[64,64,128]{2,1,0:T(8,128)(2,1)}), bf16[64,64,128]{2,1,0:T(8,128)(2,1)}, u32[]{:S(2)}, u32[]{:S(2)}) async-start(bf16[64,64,128]{2,1,0:T(8,128)(2,1)} %pool.2), calls=%async_computation.1 | async-start | bytes 2097152 | tf_op jit(solution)/shard_map/all_to_all | solution.py:427
  35.2 14.4 %pool.3 = bf16[64,64,128]{2,1,0:T(8,128)(2,1)} custom-call(s32[1]{0:T(128)} %bitcast.2.first, s32[32768]{0:T(1024)} %bitcast.42, s32[16384]{0:T(1024)} %bitcast.35, s32[128,128]{1,0:T(8,128)} %bitcast.36, bf16[8192,128]{1,0:T(8,128)(2,1)} %bitcast.31), custom_call_target="tpu_custom_call" | custom-call | bytes 36000000 | tf_op jit(solution)/shard_map/pool/pallas_call | solution.py:99
  49.6 3.5 all-to-all-done.1.arrived_low
  53.2 5.6 %all-to-all-start.2 = ((bf16[64,64,128]{2,1,0:T(8,128)(2,1)}), bf16[64,64,128]{2,1,0:T(8,128)(2,1)S(1)}, u32[]{:S(2)}, u32[]{:S(2)}) async-start(bf16[64,64,128]{2,1,0:T(8,128)(2,1)} %pool.3), calls=%async_computation.2 | async-start | bytes 2097152 | tf_op jit(solution)/shard_map/all_to_all | solution.py:427
  58.7 1.4 broadcast_in_dim.40
  60.1 16.6 %all-to-all-done.2.arrived_high = bf16[64,64,128]{2,1,0:T(8,128)(2,1)S(1)} async-done(((bf16[64,64,128]{2,1,0:T(8,128)(2,1)}), bf16[64,64,128]{2,1,0:T(8,128)(2,1)S(1)}, u32[]{:S(2)}, u32[]{:S(2)}) %all-to-all-start.2) | async-done | bytes 1048608 | tf_op jit(solution)/shard_map/all_to_all | solution.py:427
  76.8 0.0 copy-start.1
  76.8 6.4 %all-to-all-start = ((s32[32,1,256]{2,1,0:T(1,128)}), s32[32,1,256]{2,1,0:T(1,128)}, u32[]{:S(2)}, u32[]{:S(2)}) async-start(s32[32,1,256]{2,1,0:T(1,128)} %broadcast_in_dim.40), calls=%async_computation | async-start | bytes 65536 | tf_op jit(solution)/shard_map/all_to_all | solution.py:420
  83.1 0.0 copy-start.2
  83.2 6.2 %fusion.4.small = bf16[32,256,128]{2,1,0:T(8,128)(2,1)} fusion(bf16[32,512,128]{2,1,0:T(8,128)(2,1)} %param.14, s32[32,256]{1,0:T(8,128)} %bitcast.49), kind=kOutput, calls=%fused_computation.7 | convolution fusion | flops 1078984704 | bytes 6324224 | tf_op jit(solution)/shard_map/tbr,tre->tbe/dot_general | solution.py:429
  89.3 0.0 copy-done.1
  89.3 0.0 copy-done.2
  89.3 0.8 copy.14.labels
  90.1 0.0 copy-done
  90.1 0.8 dynamic-slice_reduce_fusion.sizes
  90.9 46.4 %top.1 = (bf16[32,256,128]{2,1,0:T(8,128)(2,1)}, bf16[2,64,64,128]{3,2,1,0:T(8,128)(2,1)}, bf16[2,64,64,128]{3,2,1,0:T(8,128)(2,1)}) custom-call(s32[64]{0:T(128)} %dynamic-slice_reduce_fusion.sizes, bf16[64,64,128]{2,1,0:T(8,128)(2,1)} %all-to-all-done.1.arrived_low, bf16[64,64,128]{2,1,0:T(8,128)(2,1)} %copy-done.1, bf16[32,256,128]{2,1,0:T(8,128)(2,1)} %fusion.4.small, ...), custom_call_target="tpu_custom_call" | custom-call | bytes 135000000 | tf_op jit(solution)/shard_map/top/pallas_call | solution.py:377
  137.3 0.0 all-to-all-done
  137.3 7.4 %all-to-all-start.3 = ((bf16[32,256,128]{2,1,0:T(8,128)(2,1)}), bf16[32,256,128]{2,1,0:T(8,128)(2,1)S(1)}, u32[]{:S(2)}, u32[]{:S(2)}) async-start(bf16[32,256,128]{2,1,0:T(8,128)(2,1)} %get-tuple-element.5), calls=%async_computation.3 | async-start | bytes 4194304 | tf_op jit(solution)/shard_map/all_to_all | solution.py:435
  144.7 0.0 all-gather.3.cloned.1.call-start
  144.8 30.5 %all-to-all-done.3 = bf16[32,256,128]{2,1,0:T(8,128)(2,1)S(1)} async-done(((bf16[32,256,128]{2,1,0:T(8,128)(2,1)}), bf16[32,256,128]{2,1,0:T(8,128)(2,1)S(1)}, u32[]{:S(2)}, u32[]{:S(2)}) %all-to-all-start.3) | async-done | bytes 2097184 | tf_op jit(solution)/shard_map/all_to_all | solution.py:435
  175.2 6.4 %fusion.5 = bf16[512,128]{1,0:T(8,128)(2,1)S(1)} fusion(bf16[8192,128]{1,0:T(8,128)(2,1)S(1)} %bitcast.46, s32[8192]{0:T(1024)} %bitcast.1), kind=kOutput, calls=%fused_computation.8 | convolution fusion | flops 1078001664 | bytes 2260992 | tf_op jit(solution)/shard_map/sr,se->re/dot_general | solution.py:437
  181.6 10.8 %all-gather = bf16[2048,128]{1,0:T(8,128)(2,1)S(1)} all-gather(bf16[512,128]{1,0:T(8,128)(2,1)S(1)} %fusion.5), channel_id=2, replica_groups=mesh['rep'=2,'y'=4,'zl'=2,'x'=4,'core'=2] {'x'}, dimensions={0}, use_global_device_ids=true | all-gather | bytes 655360 | tf_op jit(solution)/shard_map/all_gather | solution.py:438
  192.4 0.1 convert_reduce_fusion
  192.5 1.6 fusion.6
  194.1 0.0 all-gather.3.cloned.1.call-update
  194.1 7.4 %all-to-all-start.5 = ((bf16[128,64,128]{2,1,0:T(8,128)(2,1)}), bf16[128,64,128]{2,1,0:T(8,128)(2,1)}, u32[]{:S(2)}, u32[]{:S(2)}) async-start(bf16[128,64,128]{2,1,0:T(8,128)(2,1)} %bitcast.20), calls=%async_computation.5 | async-start | bytes 4194304 | tf_op jit(solution)/shard_map/all_to_all | solution.py:452
  201.6 79.3 %all-gather.3.cloned.1.call-done = bf16[16,512,128]{2,1,0:T(8,128)(2,1)} async-done(((bf16[1,512,128]{2,1,0:T(8,128)(2,1)}), bf16[16,512,128]{2,1,0:T(8,128)(2,1)}) %all-gather.3.cloned.1.call-update) | async-done | bytes 2097168 | tf_op jit(solution)/shard_map/all_gather | solution.py:443
  280.9 8.8 %collective-permute-start = (bf16[16,512,128]{2,1,0:T(8,128)(2,1)}, bf16[16,512,128]{2,1,0:T(8,128)(2,1)}, u32[]{:S(2)}, u32[]{:S(2)}) collective-permute-start(bf16[16,512,128]{2,1,0:T(8,128)(2,1)} %all-gather.3.cloned.1.call-done), channel_id=1, source_target_pairs={{0,1},{1,0},{2,3},{3,2},{4,5},{5,4},{6,7},{7,6},{8,9},{9,8},{10,11... | collective-permute-start | bytes 6291464 | tf_op jit(solution)/shard_map/ppermute | solution.py:444
  289.7 0.0 all-to-all-done.5.folds
  289.7 8.3 %all-to-all-start.4 = ((bf16[128,64,128]{2,1,0:T(8,128)(2,1)}), bf16[128,64,128]{2,1,0:T(8,128)(2,1)}, u32[]{:S(2)}, u32[]{:S(2)}) async-start(bf16[128,64,128]{2,1,0:T(8,128)(2,1)} %bitcast.19), calls=%async_computation.4 | async-start | bytes 4194304 | tf_op jit(solution)/shard_map/all_to_all | solution.py:452
  298.1 0.1 iota.20
  298.2 33.5 %scatter.2.rest_0_ = f32[8192,128]{1,0:T(8,128)} custom-call(s32[32768]{0:T(1024)} %bitcast.43, s32[16384]{0:T(1024)} %bitcast.37, s32[128,128]{1,0:T(8,128)} %bitcast.38, bf16[128,64,128]{2,1,0:T(8,128)(2,1)} %all-to-all-done.5.folds), custom_call_target="tpu_custom_call" | custom-call | bytes 78000000 | tf_op jit(solution)/shard_map/scatter/pallas_call | solution.py:182
  331.7 0.0 all-to-all-done.4.folds
  331.7 27.6 %scatter.3 = bf16[8192,128]{1,0:T(8,128)(2,1)} custom-call(s32[32768]{0:T(1024)} %bitcast.44, s32[16384]{0:T(1024)} %bitcast.39, s32[128,128]{1,0:T(8,128)} %bitcast.40, bf16[128,64,128]{2,1,0:T(8,128)(2,1)} %all-to-all-done.4.folds, f32[8192,128]{1,0:T(8,128)} %scatter.2.rest_0_, bf16[8192,128]{1,0:T(8,128)(2,1)} %bitcast.32), custom_call_target="tpu_custom_call" | custom-call | bytes 42000000 | tf_op jit(solution)/shard_map/scatter/pallas_call | solution.py:182
  359.3 0.0 collective-permute-done
  359.3 4.6 %bitcast_select_fusion = bf16[32,512,128]{2,1,0:T(8,128)(2,1)} fusion(pred[32]{0:T(512)(128)(4,1)S(1)} %iota.20, bf16[16,512,128]{2,1,0:T(8,128)(2,1)} %collective-permute-done, bf16[16,512,128]{2,1,0:T(8,128)(2,1)} %all-gather.3.cloned.1.call-done), kind=kLoop, calls=%fused_computation.6 | loop fusion | flops 2097152 | bytes 8388640 | tf_op jit(solution)/shard_map/jit(_where)/select_n | solution.py:447
  (2 shorter events, 0.0 us)
Async XLA Ops:
  7.2 82.9 %copy-start = (s32[64,128]{1,0:T(8,128)S(1)}, s32[64,128]{1,0:T(8,128)}, u32[]{:S(2)}) copy-start(s32[64,128]{1,0:T(8,128)} %param.16) | copy-start | bytes 98308
  24.4 28.7 %all-to-all-start.1 = ((bf16[64,64,128]{2,1,0:T(8,128)(2,1)}), bf16[64,64,128]{2,1,0:T(8,128)(2,1)}, u32[]{:S(2)}, u32[]{:S(2)}) async-start(bf16[64,64,128]{2,1,0:T(8,128)(2,1)} %pool.2), calls=%async_computation.1 | async-start | bytes 2097152 | tf_op jit(solution)/shard_map/all_to_all | solution.py:427
  53.2 23.6 %all-to-all-start.2 = ((bf16[64,64,128]{2,1,0:T(8,128)(2,1)}), bf16[64,64,128]{2,1,0:T(8,128)(2,1)S(1)}, u32[]{:S(2)}, u32[]{:S(2)}) async-start(bf16[64,64,128]{2,1,0:T(8,128)(2,1)} %pool.3), calls=%async_computation.2 | async-start | bytes 2097152 | tf_op jit(solution)/shard_map/all_to_all | solution.py:427
  76.8 12.6 %copy-start.1 = (bf16[64,64,128]{2,1,0:T(8,128)(2,1)}, bf16[64,64,128]{2,1,0:T(8,128)(2,1)S(1)}, u32[]{:S(2)}) copy-start(bf16[64,64,128]{2,1,0:T(8,128)(2,1)S(1)} %all-to-all-done.2.arrived_high) | copy-start | bytes 3145732
  76.8 60.5 %all-to-all-start = ((s32[32,1,256]{2,1,0:T(1,128)}), s32[32,1,256]{2,1,0:T(1,128)}, u32[]{:S(2)}, u32[]{:S(2)}) async-start(s32[32,1,256]{2,1,0:T(1,128)} %broadcast_in_dim.40), calls=%async_computation | async-start | bytes 65536 | tf_op jit(solution)/shard_map/all_to_all | solution.py:420
  83.1 6.2 %copy-start.2 = (s32[256]{0:T(256)S(1)}, s32[256]{0:T(256)}, u32[]{:S(2)}) copy-start(s32[256]{0:T(256)} %param.13) | copy-start | bytes 3076
  137.3 38.0 %all-to-all-start.3 = ((bf16[32,256,128]{2,1,0:T(8,128)(2,1)}), bf16[32,256,128]{2,1,0:T(8,128)(2,1)S(1)}, u32[]{:S(2)}, u32[]{:S(2)}) async-start(bf16[32,256,128]{2,1,0:T(8,128)(2,1)} %get-tuple-element.5), calls=%async_computation.3 | async-start | bytes 4194304 | tf_op jit(solution)/shard_map/all_to_all | solution.py:435
  144.7 136.2 %all-gather.3.cloned.1.call-start = ((), (), s32[]{:S(2)}) async-start(), calls=%async_computation.6 | async-start | bytes 2228224 | tf_op jit(solution)/shard_map/all_gather | solution.py:443
  194.1 95.6 %all-to-all-start.5 = ((bf16[128,64,128]{2,1,0:T(8,128)(2,1)}), bf16[128,64,128]{2,1,0:T(8,128)(2,1)}, u32[]{:S(2)}, u32[]{:S(2)}) async-start(bf16[128,64,128]{2,1,0:T(8,128)(2,1)} %bitcast.20), calls=%async_computation.5 | async-start | bytes 4194304 | tf_op jit(solution)/shard_map/all_to_all | solution.py:452
  280.9 78.3 %collective-permute-start = (bf16[16,512,128]{2,1,0:T(8,128)(2,1)}, bf16[16,512,128]{2,1,0:T(8,128)(2,1)}, u32[]{:S(2)}, u32[]{:S(2)}) collective-permute-start(bf16[16,512,128]{2,1,0:T(8,128)(2,1)} %all-gather.3.cloned.1.call-done), channel_id=1, source_target_pairs={{0,1},{1,0},{2,3},{3,2},{4,5},{5,4},{6,7},{7,6},{8,9},{9,8},{10,11... | collective-permute-start | bytes 6291464 | tf_op jit(solution)/shard_map/ppermute | solution.py:444
  289.7 41.9 %all-to-all-start.4 = ((bf16[128,64,128]{2,1,0:T(8,128)(2,1)}), bf16[128,64,128]{2,1,0:T(8,128)(2,1)}, u32[]{:S(2)}, u32[]{:S(2)}) async-start(bf16[128,64,128]{2,1,0:T(8,128)(2,1)} %bitcast.19), calls=%async_computation.4 | async-start | bytes 4194304 | tf_op jit(solution)/shard_map/all_to_all | solution.py:452
Sparse Core Ops, SparseCore 0:
  194.3 86.6 all-gather.2

commit v4 on v2

--- a/solution.py
+++ b/solution.py
@@ -40,7 +40,13 @@
 
 def pool_kernel(first, ids, flat_ends, ends, table, out, wide, rows, *, group, unroll, slots):
     dests, bags, _ = out.shape
-    wide[...] = table[...].astype(F32)
+
+    def widen(c, _):
+        span = pl.ds(pl.multiple_of(c * 256, 256), 256)
+        wide[span, :] = table[span, :].astype(F32)
+        return 0
+
+    lax.fori_loop(0, table.shape[0] // 256, widen, 0)
     rows[...] = jnp.zeros(rows.shape, F32)
 
     def one_group(g, _):
@@ -94,8 +100,13 @@
 def scatter_kernel(ids, flat_ends, ends, folds, table, out, vals, *accs, group, unroll, slots):
     dests, bags = ends.shape
     ways = len(accs)
-    for acc in accs:
-        acc[...] = jnp.zeros(acc.shape, F32)
+
+    def clear(c, _):
+        for acc in accs:
+            acc[pl.ds(pl.multiple_of(c * 128, 128), 128), :] = jnp.zeros((128, LANES), F32)
+        return 0
+
+    lax.fori_loop(0, out.shape[0] // 128, clear, 0)
 
     def one_group(g, _):
         limits = ends[pl.ds(pl.multiple_of(g * group, group), group), :]
@@ -158,11 +169,13 @@
 
 
 def top_kernel(
-    sizes, arrived, small, dense, labels, w_first, b_first, w_out,
+    sizes, arrived, small, dense, labels, w_far, b_first, w_out,
     small_out, fold_out,
-    vec, gram, feats, preact, pre_grad, pair_grad,
+    vec, gram, feats, preact, pre_grad, pair_grad, w_first, w_sem,
     *, pitch, vec_count,
 ):
+    weights = pltpu.make_async_copy(w_far, w_first, w_sem)
+    weights.start()
     feat_count, bags, width = arrived.shape
     small_count, batch, _ = small.shape
     shift = batch.bit_length() - 1
@@ -235,6 +248,7 @@
 
     lax.fori_loop(0, batch // part, pack_step, 0)
 
+    weights.wait()
     depth = pairs + width
     bulk = depth // LANES * LANES
     wide = 256
@@ -294,17 +308,14 @@
         found = []
         for n in range(together):
             spot = pl.multiple_of(base + n * pitch, 8)
-            lower = gram[pl.ds(spot, pitch), :].astype(BF16)
-            vectors = vec[pl.ds(spot, LANES), :].astype(BF16)
+            lower = gram[pl.ds(spot, pitch), :]
+            vectors = vec[pl.ds(spot, pitch), :].astype(BF16)
             found.append((lower, vectors))
         for n in range(together):
             lower, vectors = found[n]
             spot = pl.multiple_of(base + n * pitch, 8)
-            one = jnp.dot(lower, vectors, preferred_element_type=F32)
-            two = lax.dot_general(
-                lower, vectors[:pitch], (((0,), (0,)), ((), ())), preferred_element_type=F32
-            )
-            vec[pl.ds(spot, pitch), :] = one + two[:pitch]
+            both = (lower[:, :pitch] + jnp.transpose(lower)[:pitch, :]).astype(BF16)
+            vec[pl.ds(spot, pitch), :] = jnp.dot(both, vectors, preferred_element_type=F32)
         return 0
 
     lax.fori_loop(0, batch // together, grad_step, 0)
@@ -339,7 +350,7 @@
             jax.ShapeDtypeStruct((small_count, batch, width), BF16),
             jax.ShapeDtypeStruct((copies, feat_count, bags, width), BF16),
         ),
-        in_specs=[whole(pltpu.SMEM)] + [whole()] * 7,
+        in_specs=[whole(pltpu.SMEM)] + [whole()] * 4 + [whole(pl.ANY)] + [whole()] * 2,
         out_specs=(whole(), whole()),
         scratch_shapes=[
             pltpu.VMEM((batch * pitch + LANES - pitch, width), F32),
@@ -348,6 +359,8 @@
             pltpu.VMEM((batch, hidden), F32),
             pltpu.VMEM((batch, hidden), BF16),
             pltpu.VMEM((batch, up(pairs)), F32),
+            pltpu.VMEM(w_first.shape, BF16),
+            pltpu.SemaphoreType.DMA,
         ],
         compiler_params=pltpu.CompilerParams(vmem_limit_bytes=VMEM_CAP),
         cost_estimate=cost(45),
@@ -373,7 +386,8 @@
     ids = owner_row_index.reshape(-1, 8, slots // 128, 128).transpose(0, 2, 1, 3).reshape(-1)
     first = (replica * groups).astype(jnp.int32).reshape(1)
 
-    ids_sent = lax.all_to_all(small_ids.T[:, None], PLANE, 0, 0, tiled=True)
+    ids_sent = lax.all_gather(small_ids.T, PLANE)
+    ids_sent = lax.dynamic_index_in_dim(ids_sent, lax.axis_index(PLANE), 1, False)
     sizes = lax.dynamic_slice_in_dim(batch_sizes, me, 1, 1)[:, 0]
 
     pooled = pool(first, ids, flat_ends, ends, table, groups, slots)
@@ -388,7 +402,8 @@
     grads = lax.all_to_all(small_grad, PLANE, 0, 0, tiled=True).reshape(-1, LANES)
     owner_hot = (ids_sent.reshape(-1)[:, None] == jnp.arange(small_rows, dtype=jnp.int32)).astype(BF16)
     partial = jnp.einsum("sr,se->re", owner_hot, grads, preferred_element_type=F32)
-    total = lax.all_gather(partial, "x").sum(0)
+    found = lax.all_gather(partial.astype(BF16), "x")
+    total = found.astype(F32).sum(0)
     table_index = lax.axis_index(PLANE)
     mine_small = lax.dynamic_slice_in_dim(small_tables, table_index, 1, 0)[0]
     new_small = (mine_small.astype(F32) - step_size * total).astype(BF16)

time: 315 us -> 283 us (0.90)
  blocking collectives: 101 us -> 72 us
  waiting for transfers between devices: 51.1 us -> 54.7 us
    all_to_all x1 -> x0, blocking collectives: 36.5 us -> none  [step(): lax.all_to_all(small_grad, PLANE, 0, 0, tiled=True).reshape(-1, LANES)]
    all_to_all x1, waiting for transfers between devices: 0.01 us -> 29.4 us  [step(): lax.all_to_all(small_grad, PLANE, 0, 0, tiled=True).reshape(-1, LANES)]
    all_gather x1, waiting for transfers between devices: 18.6 us -> 0.02 us  [step(): ids_sent = lax.all_gather(small_ids.T, PLANE)]
    all_gather x0 -> x1, blocking collectives: none -> 11 us  [step(): found = lax.all_gather(partial.astype(BF16), 'x')]
    all_to_all x1, waiting for transfers between devices: 28.7 us -> 20.8 us  [step(): arrived = lax.all_to_all(pooled, OWNERS, 0, 0, tiled=True)]
    all_to_all x1, blocking collectives: 64.7 us -> 61 us  [step(): lax.all_to_all(folded.reshape((-1,) + folded.shape[2:]), ALL, 0, 0, tiled...]
    pallas_call x1, Pallas kernels: 50.1 us -> 46.4 us  [top(): pl.pallas_call(functools.partial(top_kernel, pitch=pitch, vec_count=vec_c...]
  transfers between devices with their start and end apart: 4 -> 4, of which waited for: 3 -> 3; matrix products, arithmetic and copies ran while one was open for 3% -> 3% of each run, Pallas kernels for 28% -> 30%
where the time goes in v4:
time: 283 us; the launch traced here: 282 us
  Pallas kernels  104 us (37%)
  blocking collectives  72 us (25%)
  waiting for transfers between devices  54.7 us (19%)
  starting transfers between devices  17.4 us (6%)
  between operations  14.1 us (5%)
  matrix products  11.7 us (4%)
  local copies, waits for them, and re-layouts  7.23 us (3%)
    all_to_all x1, blocking collectives, step(): lax.all_to_all(folded.reshape((-1,) + folded.shape[2:]), ALL, 0, 0, tiled...  61 us
    pallas_call x1, Pallas kernels, top(): pl.pallas_call(functools.partial(top_kernel, pitch=pitch, vec_count=vec_c...  46.4 us
    pallas_call x1, Pallas kernels, scatter(): pl.pallas_call(functools.partial(scatter_kernel, group=group, unroll=32,...  37 us
    all_to_all x1, waiting for transfers between devices, step(): lax.all_to_all(small_grad, PLANE, 0, 0, tiled=True).reshape(-1, LANES)  29.4 us
    all_to_all x1, waiting for transfers between devices, step(): arrived = lax.all_to_all(pooled, OWNERS, 0, 0, tiled=True)  20.8 us
    pallas_call x1, Pallas kernels, pool(): pl.pallas_call(functools.partial(pool_kernel, group=group, unroll=32, slo...  20.2 us
    all_to_all x1, starting transfers between devices, step(): arrived = lax.all_to_all(pooled, OWNERS, 0, 0, tiled=True)  11.3 us
    all_gather x1, blocking collectives, step(): found = lax.all_gather(partial.astype(BF16), 'x')  11 us
  transfers between devices with their start and end apart: 4, of which 3 were waited for; matrix products, arithmetic and copies ran while one was open for 3% of the time, Pallas kernels for 30%

profile of v4, /device:TPU:1, one launch (start us, length us, event | category | flops | bytes accessed | tf_op | source)
XLA Modules:
  0.0 282.4 jit_solution(7831935633069921408)
XLA Ops:
  7.2 0.0 copy-start
  7.2 20.2 %pool.1 = bf16[64,128,128]{2,1,0:T(8,128)(2,1)} custom-call(s32[1]{0:T(128)} %bitcast.3.first, s32[32768]{0:T(1024)} %bitcast.36, s32[16384]{0:T(1024)} %bitcast.32, s32[128,128]{1,0:T(8,128)} %bitcast.33, bf16[8192,128]{1,0:T(8,128)(2,1)} %bitcast.26), custom_call_target="tpu_custom_call" | custom-call | bytes 48000000 | tf_op jit(solution)/shard_map/pool/pallas_call | solution.py:85
  27.4 0.0 copy-start.1
  27.4 11.3 %all-to-all-start = ((bf16[64,128,128]{2,1,0:T(8,128)(2,1)}), bf16[64,128,128]{2,1,0:T(8,128)(2,1)}, u32[]{:S(2)}, u32[]{:S(2)}) async-start(bf16[64,128,128]{2,1,0:T(8,128)(2,1)} %pool.1), calls=%async_computation | async-start | bytes 4194304 | tf_op jit(solution)/shard_map/all_to_all | solution.py:394
  38.7 0.0 all-gather.7.cloned.1.call-start
  38.7 0.7 all-gather.7.cloned.1.call-update
  39.4 0.0 copy-done.1
  39.4 0.0 copy-start.2
  39.5 6.1 %fusion.4.small = bf16[32,256,128]{2,1,0:T(8,128)(2,1)} fusion(bf16[32,512,128]{2,1,0:T(8,128)(2,1)} %param.14, s32[32,256]{1,0:T(8,128)S(1)} %bitcast.39), kind=kOutput, calls=%fused_computation.6 | convolution fusion | flops 1078984704 | bytes 6324224 | tf_op jit(solution)/shard_map/tbr,tre->tbe/dot_general | solution.py:396
  45.6 0.0 copy-done.2
  45.6 0.8 copy.14.labels
  46.4 0.0 copy-done
  46.4 0.8 dynamic-slice_reduce_fusion.sizes
  47.1 20.8 %all-to-all-done.arrived = bf16[64,128,128]{2,1,0:T(8,128)(2,1)} async-done(((bf16[64,128,128]{2,1,0:T(8,128)(2,1)}), bf16[64,128,128]{2,1,0:T(8,128)(2,1)}, u32[]{:S(2)}, u32[]{:S(2)}) %all-to-all-start) | async-done | bytes 2097184 | tf_op jit(solution)/shard_map/all_to_all | solution.py:394
  67.9 46.4 %top.1 = (bf16[32,256,128]{2,1,0:T(8,128)(2,1)}, bf16[2,64,128,128]{3,2,1,0:T(8,128)(2,1)}) custom-call(s32[64]{0:T(128)} %dynamic-slice_reduce_fusion.sizes, bf16[64,128,128]{2,1,0:T(8,128)(2,1)} %all-to-all-done.arrived, bf16[32,256,128]{2,1,0:T(8,128)(2,1)} %fusion.4.small, bf16[256,128]{1,0:T(8,128)(2,1)} %dense.1, s32[256,1]{1,0:T(8,128)} %copy.14.labels, ...), custom_call_target="tpu_custom_call" | custom-call | bytes 135000000 | tf_op jit(solution)/shard_map/top/pallas_call | solution.py:347
  114.3 6.0 %all-to-all-start.1 = ((bf16[32,256,128]{2,1,0:T(8,128)(2,1)}), bf16[32,256,128]{2,1,0:T(8,128)(2,1)S(1)}, u32[]{:S(2)}, u32[]{:S(2)}) async-start(bf16[32,256,128]{2,1,0:T(8,128)(2,1)} %get-tuple-element.4), calls=%async_computation.1 | async-start | bytes 4194304 | tf_op jit(solution)/shard_map/all_to_all | solution.py:402
  120.4 0.0 all-gather.5.cloned.1.call-start
  120.4 0.0 all-gather.7.cloned.1.call-done
  120.5 1.0 constant_dynamic-slice_fusion
  121.4 29.4 %all-to-all-done.1 = bf16[32,256,128]{2,1,0:T(8,128)(2,1)S(1)} async-done(((bf16[32,256,128]{2,1,0:T(8,128)(2,1)}), bf16[32,256,128]{2,1,0:T(8,128)(2,1)S(1)}, u32[]{:S(2)}, u32[]{:S(2)}) %all-to-all-start.1) | async-done | bytes 2097184 | tf_op jit(solution)/shard_map/all_to_all | solution.py:402
  150.9 5.6 %fusion.5 = bf16[512,128]{1,0:T(8,128)(2,1)S(1)} fusion(bf16[8192,128]{1,0:T(8,128)(2,1)S(1)} %bitcast.30, s32[8192]{0:T(1024)S(1)} %bitcast.40), kind=kOutput, calls=%fused_computation.7 | convolution fusion | flops 1078001664 | bytes 2260992 | tf_op jit(solution)/shard_map/sr,se->re/dot_general | solution.py:404
  156.5 11.0 %all-gather.1 = bf16[2048,128]{1,0:T(8,128)(2,1)S(1)} all-gather(bf16[512,128]{1,0:T(8,128)(2,1)S(1)} %fusion.5), channel_id=3, replica_groups=mesh['rep'=2,'y'=4,'zl'=2,'x'=4,'core'=2] {'x'}, dimensions={0}, use_global_device_ids=true | all-gather | bytes 655360 | tf_op jit(solution)/shard_map/all_gather | solution.py:405
  167.5 0.1 convert_reduce_fusion
  167.6 1.6 fusion.6
  169.2 0.0 all-gather.5.cloned.1.call-update
  169.2 61.0 %all_to_all.15.folds = bf16[128,128,128]{2,1,0:T(8,128)(2,1)} all-to-all(bf16[128,128,128]{2,1,0:T(8,128)(2,1)} %bitcast.28), channel_id=1, replica_groups=mesh['rep'=2,'y'=4,'zl'=2,'x'=4,'core'=2] {'rep','y','zl','x','core'}, dimensions={0} | all-to-all | bytes 8388608 | tf_op jit(solution)/shard_map/all_to_all | solution.py:412
  230.2 37.0 %scatter.1 = bf16[8192,128]{1,0:T(8,128)(2,1)} custom-call(s32[32768]{0:T(1024)} %bitcast.37, s32[16384]{0:T(1024)} %bitcast.34, s32[128,128]{1,0:T(8,128)} %bitcast.35, bf16[128,128,128]{2,1,0:T(8,128)(2,1)} %all_to_all.15.folds, bf16[8192,128]{1,0:T(8,128)(2,1)} %bitcast.27), custom_call_target="tpu_custom_call" | custom-call | bytes 84000000 | tf_op jit(solution)/shard_map/scatter/pallas_call | solution.py:158
  267.2 3.7 %all-gather.5.cloned.1.call-done = bf16[32,512,128]{2,1,0:T(8,128)(2,1)} async-done(((bf16[1,512,128]{2,1,0:T(8,128)(2,1)}), bf16[32,512,128]{2,1,0:T(8,128)(2,1)}) %all-gather.5.cloned.1.call-update) | async-done | bytes 4194320 | tf_op jit(solution)/shard_map/all_gather | solution.py:410
  270.9 4.7 %copy.16 = bf16[32,512,128]{2,1,0:T(8,128)(2,1)} copy(bf16[32,512,128]{2,1,0:T(8,128)(2,1)} %all-gather.5.cloned.1.call-done) | data formatting | bytes 8388608
Async XLA Ops:
  7.2 39.2 %copy-start = (s32[64,128]{1,0:T(8,128)S(1)}, s32[64,128]{1,0:T(8,128)}, u32[]{:S(2)}) copy-start(s32[64,128]{1,0:T(8,128)} %param.16) | copy-start | bytes 98308
  27.4 12.0 %copy-start.1 = (s32[256,32]{0,1:T(8,128)S(1)}, s32[256,32]{0,1:T(8,128)}, u32[]{:S(2)}) copy-start(s32[256,32]{0,1:T(8,128)} %param.12) | copy-start | bytes 98308
  27.4 40.5 %all-to-all-start = ((bf16[64,128,128]{2,1,0:T(8,128)(2,1)}), bf16[64,128,128]{2,1,0:T(8,128)(2,1)}, u32[]{:S(2)}, u32[]{:S(2)}) async-start(bf16[64,128,128]{2,1,0:T(8,128)(2,1)} %pool.1), calls=%async_computation | async-start | bytes 4194304 | tf_op jit(solution)/shard_map/all_to_all | solution.py:394
  38.7 81.8 %all-gather.7.cloned.1.call-start = ((), (), s32[]{:S(2)}) async-start(), calls=%async_computation.4 | async-start | bytes 1081344 | tf_op jit(solution)/shard_map/all_gather | solution.py:389
  39.4 6.1 %copy-start.2 = (s32[256]{0:T(256)S(1)}, s32[256]{0:T(256)}, u32[]{:S(2)}) copy-start(s32[256]{0:T(256)} %param.13) | copy-start | bytes 3076
  114.3 36.6 %all-to-all-start.1 = ((bf16[32,256,128]{2,1,0:T(8,128)(2,1)}), bf16[32,256,128]{2,1,0:T(8,128)(2,1)S(1)}, u32[]{:S(2)}, u32[]{:S(2)}) async-start(bf16[32,256,128]{2,1,0:T(8,128)(2,1)} %get-tuple-element.4), calls=%async_computation.1 | async-start | bytes 4194304 | tf_op jit(solution)/shard_map/all_to_all | solution.py:402
  120.4 150.6 %all-gather.5.cloned.1.call-start = ((), (), s32[]{:S(2)}) async-start(), calls=%async_computation.3 | async-start | bytes 4325376 | tf_op jit(solution)/shard_map/all_gather | solution.py:410
Sparse Core Ops, SparseCore 0:
  41.2 65.1 all-gather.6
  169.4 101.5 all-gather.4

commit v5 on v4

--- a/solution.py
+++ b/solution.py
@@ -38,8 +38,37 @@
     return (((d >> 3) * (slots // 128) + (k >> 7)) << 10) + ((d & 7) << 7) + (k & 127)
 
 
-def pool_kernel(first, ids, flat_ends, ends, table, out, wide, rows, *, group, unroll, slots):
-    dests, bags, _ = out.shape
+def pool_kernel(
+    ids, ends, table, arrived, wide, rows, pooled, send_sem, recv_sem, self_sem, *, group, unroll, slots
+):
+    dests = arrived.shape[0]
+    groups = dests // group
+    row_index = lax.axis_index("y") * lax.axis_size("zl") + lax.axis_index("zl")
+    mine = row_index * group + lax.axis_index("x") * lax.axis_size("core") + lax.axis_index("core")
+    first = lax.axis_index("rep") * dests
+
+    def place(g, i):
+        return {
+            "y": g // lax.axis_size("zl"),
+            "zl": lax.rem(g, lax.axis_size("zl")),
+            "x": i // lax.axis_size("core"),
+            "core": i % lax.axis_size("core"),
+        }
+
+    barrier = pltpu.get_barrier_semaphore()
+
+    def greet(g, _):
+        for i in range(group):
+
+            @pl.when(g * group + i != mine)
+            def _():
+                pl.semaphore_signal(
+                    barrier, 1, device_id=place(g, i), device_id_type=pl.DeviceIdType.MESH
+                )
+
+        return 0
+
+    lax.fori_loop(0, groups, greet, 0)
 
     def widen(c, _):
         span = pl.ds(pl.multiple_of(c * 256, 256), 256)
@@ -47,54 +76,100 @@
         return 0
 
     lax.fori_loop(0, table.shape[0] // 256, widen, 0)
-    rows[...] = jnp.zeros(rows.shape, F32)
-
-    def one_group(g, _):
+    pl.semaphore_wait(barrier, dests - 1)
+
+    def turn(step):
+        return lax.rem(row_index + step, groups)
+
+    def send(step):
+        g = turn(step)
+        for i in range(group):
+            d = g * group + i
+
+            @pl.when(d != mine)
+            def _():
+                pltpu.make_async_remote_copy(
+                    src_ref=pooled.at[d],
+                    dst_ref=arrived.at[mine],
+                    send_sem=send_sem,
+                    recv_sem=recv_sem,
+                    device_id=place(g, i),
+                    device_id_type=pl.DeviceIdType.MESH,
+                ).start()
+
+    def one_group(step, _):
+        g = turn(step)
+
         def one_dest(i, _):
-            d = first[0] + g * group + i
+            d = first + g * group + i
             row = i * slots
 
             def chunk(c, _):
                 start = slot_base(d, c * unroll, slots)
-                place = row + c * unroll
+                spot = row + c * unroll
                 for u in range(unroll):
-                    rows[pl.ds(place + u, 1), :] = wide[pl.ds(ids[start + u], 1), :]
+                    rows[pl.ds(spot + u, 1), :] = wide[pl.ds(ids[start + u], 1), :]
                 return 0
 
-            used = flat_ends[d * bags + bags - 1]
-            lax.fori_loop(0, (used + unroll - 1) >> (unroll.bit_length() - 1), chunk, 0)
+            lax.fori_loop(0, slots // unroll, chunk, 0)
             return 0
 
         lax.fori_loop(0, group, one_dest, 0)
-        limits = ends[pl.ds(pl.multiple_of(first[0] + g * group, group), group), :]
+
+        @pl.when(step > 0)
+        def _():
+            send(step - 1)
+
+        limits = ends[pl.ds(pl.multiple_of(first + g * group, group), group), :]
         for i in range(group):
             mask = bag_mask(limits[i : i + 1], slots)
             taken = rows[i * slots : (i + 1) * slots, :].astype(BF16)
             total = lax.dot_general(
                 mask, taken, (((0,), (0,)), ((), ())), preferred_element_type=F32
             )
-            out[g * group + i] = total.astype(BF16)
-        return 0
-
-    lax.fori_loop(0, dests // group, one_group, 0)
-
-
-def pool(first, ids, flat_ends, ends, table, dests, slots):
+            pooled[g * group + i] = total.astype(BF16)
+        return 0
+
+    lax.fori_loop(0, groups, one_group, 0)
+    own = pltpu.make_async_copy(pooled.at[mine], arrived.at[mine], self_sem)
+    own.start()
+    send(groups - 1)
+    own.wait()
+    whole_span = pl.ds(0, dests - 1)
+    every = pltpu.make_async_remote_copy(
+        src_ref=pooled.at[whole_span],
+        dst_ref=arrived.at[whole_span],
+        send_sem=send_sem,
+        recv_sem=recv_sem,
+        device_id=place(lax.rem(row_index + 1, groups), 0),
+        device_id_type=pl.DeviceIdType.MESH,
+    )
+    every.wait_send()
+    every.wait_recv()
+
+
+def pool_and_send(ids, ends, table, dests, slots):
     bags = ends.shape[1]
     group = 8
     return pl.pallas_call(
-        functools.partial(pool_kernel, group=group, unroll=32, slots=slots),
+        functools.partial(pool_kernel, group=group, unroll=64, slots=slots),
         out_shape=jax.ShapeDtypeStruct((dests, bags, LANES), BF16),
-        in_specs=[whole(pltpu.SMEM)] * 3 + [whole()] * 2,
-        out_specs=whole(),
+        in_specs=[whole(pltpu.SMEM)] + [whole()] * 2,
+        out_specs=whole(pl.ANY),
         scratch_shapes=[
             pltpu.VMEM(table.shape, F32),
             pltpu.VMEM((group * slots, LANES), F32),
+            pltpu.VMEM((dests, bags, LANES), BF16),
+            pltpu.SemaphoreType.DMA,
+            pltpu.SemaphoreType.DMA,
+            pltpu.SemaphoreType.DMA,
         ],
-        compiler_params=pltpu.CompilerParams(vmem_limit_bytes=VMEM_CAP),
-        cost_estimate=cost(16),
+        compiler_params=pltpu.CompilerParams(
+            vmem_limit_bytes=VMEM_CAP, collective_id=0, has_side_effects=True
+        ),
+        cost_estimate=cost(32),
         name="pool",
-    )(first, ids, flat_ends, ends, table)
+    )(ids, ends, table)
 
 
 def scatter_kernel(ids, flat_ends, ends, folds, table, out, vals, *accs, group, unroll, slots):
@@ -376,7 +451,6 @@
     for name in OWNERS:
         groups = groups * lax.axis_size(name)
     copies = lax.axis_size("rep")
-    replica = lax.axis_index("rep")
     me = lax.axis_index(ALL)
     small_rows = small_tables.shape[1]
     table = large_tables[0]
@@ -384,14 +458,13 @@
     slots = owner_row_index.shape[2]
     flat_ends = ends.reshape(-1)
     ids = owner_row_index.reshape(-1, 8, slots // 128, 128).transpose(0, 2, 1, 3).reshape(-1)
-    first = (replica * groups).astype(jnp.int32).reshape(1)
-
-    ids_sent = lax.all_gather(small_ids.T, PLANE)
+
+    sizes = lax.dynamic_slice_in_dim(batch_sizes, me, 1, 1)[:, 0]
+
+    arrived = pool_and_send(ids, ends, table, groups, slots)
+    later_ids, arrived = lax.optimization_barrier((small_ids, arrived))
+    ids_sent = lax.all_gather(later_ids.T, PLANE)
     ids_sent = lax.dynamic_index_in_dim(ids_sent, lax.axis_index(PLANE), 1, False)
-    sizes = lax.dynamic_slice_in_dim(batch_sizes, me, 1, 1)[:, 0]
-
-    pooled = pool(first, ids, flat_ends, ends, table, groups, slots)
-    arrived = lax.all_to_all(pooled, OWNERS, 0, 0, tiled=True)
     hot = (small_ids.T[:, :, None] == jnp.arange(small_rows, dtype=jnp.int32)).astype(BF16)
     small = jnp.einsum("tbr,tre->tbe", hot, small_tables, preferred_element_type=F32).astype(BF16)
 

time: 283 us -> 281 us (level)
  Pallas kernels: 104 us -> 134 us
  waiting for transfers between devices: 54.7 us -> 32.9 us
  starting transfers between devices: 17.4 us -> 7.2 us
    pallas_call x1, Pallas kernels: 20.2 us -> 50.3 us  [pool_and_send(): pl.pallas_call(functools.partial(pool_kernel, group=group, unroll=64, slo...]
    all_to_all x1 -> x0, waiting for transfers between devices: 20.8 us -> none  [step(): arrived = lax.all_to_all(pooled, OWNERS, 0, 0, tiled=True)]
    all_to_all x1 -> x0, starting transfers between devices: 11.3 us -> none  [step(): arrived = lax.all_to_all(pooled, OWNERS, 0, 0, tiled=True)]
  transfers between devices with their start and end apart: 4 -> 3, of which waited for: 3 -> 2; matrix products, arithmetic and copies ran while one was open for 3% -> 3% of each run, Pallas kernels for 30% -> 30%
where the time goes in v5:
time: 281 us; the launch traced here: 280 us
  Pallas kernels  134 us (48%)
  blocking collectives  72 us (26%)
  waiting for transfers between devices  32.9 us (12%)
  between operations  14.1 us (5%)
  matrix products  11.8 us (4%)
  starting transfers between devices  7.2 us (3%)
  local copies, waits for them, and re-layouts  7.16 us (3%)
    all_to_all x1, blocking collectives, step(): lax.all_to_all(folded.reshape((-1,) + folded.shape[2:]), ALL, 0, 0, tiled...  61.4 us
    pallas_call x1, Pallas kernels, pool_and_send(): pl.pallas_call(functools.partial(pool_kernel, group=group, unroll=64, slo...  50.3 us
    pallas_call x1, Pallas kernels, top(): pl.pallas_call(functools.partial(top_kernel, pitch=pitch, vec_count=vec_c...  46.4 us
    pallas_call x1, Pallas kernels, scatter(): pl.pallas_call(functools.partial(scatter_kernel, group=group, unroll=32,...  37 us
    all_to_all x1, waiting for transfers between devices, step(): lax.all_to_all(small_grad, PLANE, 0, 0, tiled=True).reshape(-1, LANES)  29.4 us
    all_gather x1, blocking collectives, step(): found = lax.all_gather(partial.astype(BF16), 'x')  10.6 us
    all_to_all x1, starting transfers between devices, step(): lax.all_to_all(small_grad, PLANE, 0, 0, tiled=True).reshape(-1, LANES)  7.12 us
    dot_general x1, matrix products, step(): jnp.einsum('tbr,tre->tbe', hot, small_tables, preferred_element_type=F32)  6.15 us
  transfers between devices with their start and end apart: 3, of which 2 were waited for; matrix products, arithmetic and copies ran while one was open for 3% of the time, Pallas kernels for 30%

profile of v5, /device:TPU:1, one launch (start us, length us, event | category | flops | bytes accessed | tf_op | source)
XLA Modules:
  0.0 280.5 jit_solution(5626966539485174401)
XLA Ops:
  7.2 0.0 copy-start
  7.2 0.0 all-gather.7.cloned.1.call-start
  7.2 50.3 %pool.1.arrived = bf16[64,128,128]{2,1,0:T(8,128)(2,1)} custom-call(s32[32768]{0:T(1024)} %bitcast.35, s32[128,128]{1,0:T(8,128)} %bitcast.32, bf16[8192,128]{1,0:T(8,128)(2,1)} %bitcast.26), custom_call_target="tpu_custom_call" | custom-call | bytes 96000000 | tf_op jit(solution)/shard_map/pool/pallas_call | solution.py:154
  57.6 0.0 all-gather.7.cloned.1.call-update
  57.6 0.0 copy-start.1
  57.6 6.2 %fusion.4.small = bf16[32,256,128]{2,1,0:T(8,128)(2,1)} fusion(bf16[32,512,128]{2,1,0:T(8,128)(2,1)} %param.14, s32[32,256]{1,0:T(8,128)} %bitcast.38), kind=kOutput, calls=%fused_computation.6 | convolution fusion | flops 1078984704 | bytes 6324224 | tf_op jit(solution)/shard_map/tbr,tre->tbe/dot_general | solution.py:469
  63.7 0.0 copy-done.1
  63.8 0.8 copy.14.labels
  64.5 0.0 copy-done
  64.5 0.7 dynamic-slice_reduce_fusion.sizes
  65.3 46.4 %top.1 = (bf16[32,256,128]{2,1,0:T(8,128)(2,1)}, bf16[2,64,128,128]{3,2,1,0:T(8,128)(2,1)}) custom-call(s32[64]{0:T(128)} %dynamic-slice_reduce_fusion.sizes, bf16[64,128,128]{2,1,0:T(8,128)(2,1)} %pool.1.arrived, bf16[32,256,128]{2,1,0:T(8,128)(2,1)} %fusion.4.small, bf16[256,128]{1,0:T(8,128)(2,1)} %dense.1, s32[256,1]{1,0:T(8,128)} %copy.14.labels, ...), custom_call_target="tpu_custom_call" | custom-call | bytes 135000000 | tf_op jit(solution)/shard_map/top/pallas_call | solution.py:422
  111.6 7.1 %all-to-all-start = ((bf16[32,256,128]{2,1,0:T(8,128)(2,1)}), bf16[32,256,128]{2,1,0:T(8,128)(2,1)S(1)}, u32[]{:S(2)}, u32[]{:S(2)}) async-start(bf16[32,256,128]{2,1,0:T(8,128)(2,1)} %get-tuple-element.8), calls=%async_computation | async-start | bytes 4194304 | tf_op jit(solution)/shard_map/all_to_all | solution.py:475
  118.8 0.0 all-gather.5.cloned.1.call-start
  118.8 0.0 all-gather.7.cloned.1.call-done
  118.8 1.0 constant_dynamic-slice_fusion
  119.8 29.4 %all-to-all-done = bf16[32,256,128]{2,1,0:T(8,128)(2,1)S(1)} async-done(((bf16[32,256,128]{2,1,0:T(8,128)(2,1)}), bf16[32,256,128]{2,1,0:T(8,128)(2,1)S(1)}, u32[]{:S(2)}, u32[]{:S(2)}) %all-to-all-start) | async-done | bytes 2097184 | tf_op jit(solution)/shard_map/all_to_all | solution.py:475
  149.3 5.6 %fusion.5 = bf16[512,128]{1,0:T(8,128)(2,1)S(1)} fusion(bf16[8192,128]{1,0:T(8,128)(2,1)S(1)} %bitcast.30, s32[8192]{0:T(1024)S(1)} %bitcast.39), kind=kOutput, calls=%fused_computation.7 | convolution fusion | flops 1078001664 | bytes 2260992 | tf_op jit(solution)/shard_map/sr,se->re/dot_general | solution.py:477
  154.9 10.6 %all-gather.1 = bf16[2048,128]{1,0:T(8,128)(2,1)S(1)} all-gather(bf16[512,128]{1,0:T(8,128)(2,1)S(1)} %fusion.5), channel_id=3, replica_groups=mesh['rep'=2,'y'=4,'zl'=2,'x'=4,'core'=2] {'x'}, dimensions={0}, use_global_device_ids=true | all-gather | bytes 655360 | tf_op jit(solution)/shard_map/all_gather | solution.py:478
  165.6 0.1 convert_reduce_fusion
  165.6 1.6 fusion.6
  167.2 0.0 all-gather.5.cloned.1.call-update
  167.2 61.4 %all_to_all.10.folds = bf16[128,128,128]{2,1,0:T(8,128)(2,1)} all-to-all(bf16[128,128,128]{2,1,0:T(8,128)(2,1)} %bitcast.28), channel_id=1, replica_groups=mesh['rep'=2,'y'=4,'zl'=2,'x'=4,'core'=2] {'rep','y','zl','x','core'}, dimensions={0} | all-to-all | bytes 8388608 | tf_op jit(solution)/shard_map/all_to_all | solution.py:485
  228.6 37.0 %scatter.1 = bf16[8192,128]{1,0:T(8,128)(2,1)} custom-call(s32[32768]{0:T(1024)} %bitcast.36, s32[16384]{0:T(1024)} %bitcast.34, s32[128,128]{1,0:T(8,128)} %bitcast.33, bf16[128,128,128]{2,1,0:T(8,128)(2,1)} %all_to_all.10.folds, bf16[8192,128]{1,0:T(8,128)(2,1)} %bitcast.27), custom_call_target="tpu_custom_call" | custom-call | bytes 84000000 | tf_op jit(solution)/shard_map/scatter/pallas_call | solution.py:233
  265.6 3.4 %all-gather.5.cloned.1.call-done = bf16[32,512,128]{2,1,0:T(8,128)(2,1)} async-done(((bf16[1,512,128]{2,1,0:T(8,128)(2,1)}), bf16[32,512,128]{2,1,0:T(8,128)(2,1)}) %all-gather.5.cloned.1.call-update) | async-done | bytes 4194320 | tf_op jit(solution)/shard_map/all_gather | solution.py:483
  269.0 4.7 %copy.16 = bf16[32,512,128]{2,1,0:T(8,128)(2,1)} copy(bf16[32,512,128]{2,1,0:T(8,128)(2,1)} %all-gather.5.cloned.1.call-done) | data formatting | bytes 8388608
Async XLA Ops:
  7.2 57.4 %copy-start = (s32[64,128]{1,0:T(8,128)S(1)}, s32[64,128]{1,0:T(8,128)}, u32[]{:S(2)}) copy-start(s32[64,128]{1,0:T(8,128)} %param.16) | copy-start | bytes 98308
  7.2 111.7 %all-gather.7.cloned.1.call-start = ((), (), s32[]{:S(2)}) async-start(), calls=%async_computation.3 | async-start | bytes 1081344 | tf_op jit(solution)/shard_map/all_gather | solution.py:466
  57.6 6.2 %copy-start.1 = (s32[256]{0:T(256)S(1)}, s32[256]{0:T(256)}, u32[]{:S(2)}) copy-start(s32[256]{0:T(256)} %param.13) | copy-start | bytes 3076
  111.6 37.7 %all-to-all-start = ((bf16[32,256,128]{2,1,0:T(8,128)(2,1)}), bf16[32,256,128]{2,1,0:T(8,128)(2,1)S(1)}, u32[]{:S(2)}, u32[]{:S(2)}) async-start(bf16[32,256,128]{2,1,0:T(8,128)(2,1)} %get-tuple-element.8), calls=%async_computation | async-start | bytes 4194304 | tf_op jit(solution)/shard_map/all_to_all | solution.py:475
  118.8 150.2 %all-gather.5.cloned.1.call-start = ((), (), s32[]{:S(2)}) async-start(), calls=%async_computation.2 | async-start | bytes 4325376 | tf_op jit(solution)/shard_map/all_gather | solution.py:483
Sparse Core Ops, SparseCore 0:
  57.7 55.9 all-gather.6
  167.4 101.5 all-gather.4

commit v6 on v5

--- a/solution.py
+++ b/solution.py
@@ -39,7 +39,8 @@
 
 
 def pool_kernel(
-    ids, ends, table, arrived, wide, rows, pooled, send_sem, recv_sem, self_sem, *, group, unroll, slots
+    ids, ends, small_ids, table, small_far, arrived, small,
+    wide, rows, pooled, small_tables, send_sem, recv_sem, self_sem, small_sem, *, group, unroll, slots
 ):
     dests = arrived.shape[0]
     groups = dests // group
@@ -55,6 +56,8 @@
             "core": i % lax.axis_size("core"),
         }
 
+    tables = pltpu.make_async_copy(small_far, small_tables, small_sem)
+    tables.start()
     barrier = pltpu.get_barrier_semaphore()
 
     def greet(g, _):
@@ -78,8 +81,11 @@
     lax.fori_loop(0, table.shape[0] // 256, widen, 0)
     pl.semaphore_wait(barrier, dests - 1)
 
+    half = groups // 2
+
     def turn(step):
-        return lax.rem(row_index + step, groups)
+        y = lax.rem(lax.axis_index("y") + 2 + 3 * step, half)
+        return y * 2 + lax.rem(lax.axis_index("zl") + 1 + step // half, 2)
 
     def send(step):
         g = turn(step)
@@ -134,6 +140,14 @@
     own = pltpu.make_async_copy(pooled.at[mine], arrived.at[mine], self_sem)
     own.start()
     send(groups - 1)
+    tables.wait()
+    count, small_rows, _ = small_tables.shape
+    batch = small_ids.shape[1]
+    columns = jnp.transpose(small_ids[...].astype(F32))
+    row = lax.broadcasted_iota(jnp.int32, (batch, small_rows), 1).astype(F32)
+    for t in range(count):
+        hot = jnp.where(columns[:, t : t + 1] == row, 1.0, 0.0).astype(BF16)
+        small[t] = jnp.dot(hot, small_tables[t], preferred_element_type=F32).astype(BF16)
     own.wait()
     whole_span = pl.ds(0, dests - 1)
     every = pltpu.make_async_remote_copy(
@@ -148,18 +162,23 @@
     every.wait_recv()
 
 
-def pool_and_send(ids, ends, table, dests, slots):
+def pool_and_send(ids, ends, small_ids, table, small_tables, dests, slots):
     bags = ends.shape[1]
     group = 8
     return pl.pallas_call(
         functools.partial(pool_kernel, group=group, unroll=64, slots=slots),
-        out_shape=jax.ShapeDtypeStruct((dests, bags, LANES), BF16),
-        in_specs=[whole(pltpu.SMEM)] + [whole()] * 2,
-        out_specs=whole(pl.ANY),
+        out_shape=(
+            jax.ShapeDtypeStruct((dests, bags, LANES), BF16),
+            jax.ShapeDtypeStruct(small_ids.shape + (LANES,), BF16),
+        ),
+        in_specs=[whole(pltpu.SMEM)] + [whole()] * 3 + [whole(pl.ANY)],
+        out_specs=(whole(pl.ANY), whole()),
         scratch_shapes=[
             pltpu.VMEM(table.shape, F32),
             pltpu.VMEM((group * slots, LANES), F32),
             pltpu.VMEM((dests, bags, LANES), BF16),
+            pltpu.VMEM(small_tables.shape, BF16),
+            pltpu.SemaphoreType.DMA,
             pltpu.SemaphoreType.DMA,
             pltpu.SemaphoreType.DMA,
             pltpu.SemaphoreType.DMA,
@@ -169,7 +188,7 @@
         ),
         cost_estimate=cost(32),
         name="pool",
-    )(ids, ends, table)
+    )(ids, ends, small_ids, table, small_tables)
 
 
 def scatter_kernel(ids, flat_ends, ends, folds, table, out, vals, *accs, group, unroll, slots):
@@ -461,13 +480,12 @@
 
     sizes = lax.dynamic_slice_in_dim(batch_sizes, me, 1, 1)[:, 0]
 
-    arrived = pool_and_send(ids, ends, table, groups, slots)
+    arrived, small = pool_and_send(
+        ids, ends, small_ids.T, table, small_tables, groups, slots
+    )
     later_ids, arrived = lax.optimization_barrier((small_ids, arrived))
     ids_sent = lax.all_gather(later_ids.T, PLANE)
     ids_sent = lax.dynamic_index_in_dim(ids_sent, lax.axis_index(PLANE), 1, False)
-    hot = (small_ids.T[:, :, None] == jnp.arange(small_rows, dtype=jnp.int32)).astype(BF16)
-    small = jnp.einsum("tbr,tre->tbe", hot, small_tables, preferred_element_type=F32).astype(BF16)
-
     small_grad, folded = top(
         sizes, arrived, small, dense, labels[:, None], w_first, b_first[None], w_out[None], copies
     )

time: 281 us -> 276 us (0.982)
  matrix products: 11.8 us -> 5.63 us
  waiting for transfers between devices: 32.9 us -> 29.6 us
    dot_general x1 -> x0, matrix products: 6.15 us -> none  [step(): jnp.einsum('tbr,tre->tbe', hot, small_tables, preferred_element_type=F32)]
    all_gather x1, waiting for transfers between devices: 3.39 us -> 0.13 us  [step(): small_new = lax.all_gather(new_small, PLANE)]
  transfers between devices with their start and end apart: 3 -> 3, of which waited for: 2 -> 3; matrix products, arithmetic and copies ran while one was open for 3% -> 1% of each run, Pallas kernels for 30% -> 30%
where the time goes in v6:
time: 276 us; the launch traced here: 274 us
  Pallas kernels  136 us (49%)
  blocking collectives  73 us (26%)
  waiting for transfers between devices  29.6 us (11%)
  between operations  14.1 us (5%)
  starting transfers between devices  7.18 us (3%)
  local copies, waits for them, and re-layouts  7.16 us (3%)
  matrix products  5.63 us (2%)
    all_to_all x1, blocking collectives, step(): lax.all_to_all(folded.reshape((-1,) + folded.shape[2:]), ALL, 0, 0, tiled...  62.8 us
    pallas_call x1, Pallas kernels, pool_and_send(): pl.pallas_call(functools.partial(pool_kernel, group=group, unroll=64, slo...  52.5 us
    pallas_call x1, Pallas kernels, top(): pl.pallas_call(functools.partial(top_kernel, pitch=pitch, vec_count=vec_c...  46.4 us
    pallas_call x1, Pallas kernels, scatter(): pl.pallas_call(functools.partial(scatter_kernel, group=group, unroll=32,...  37 us
    all_to_all x1, waiting for transfers between devices, step(): lax.all_to_all(small_grad, PLANE, 0, 0, tiled=True).reshape(-1, LANES)  27.5 us
    all_gather x1, blocking collectives, step(): found = lax.all_gather(partial.astype(BF16), 'x')  10.2 us
    all_to_all x1, starting transfers between devices, step(): lax.all_to_all(small_grad, PLANE, 0, 0, tiled=True).reshape(-1, LANES)  7.1 us
    dot_general x1, matrix products, step(): jnp.einsum('sr,se->re', owner_hot, grads, preferred_element_type=F32)  5.63 us
  transfers between devices with their start and end apart: 3, of which 3 were waited for; matrix products, arithmetic and copies ran while one was open for 1% of the time, Pallas kernels for 30%

profile of v6, /device:TPU:1, one launch (start us, length us, event | category | flops | bytes accessed | tf_op | source)
XLA Modules:
  0.0 274.2 jit_solution(7502345791855122731)
XLA Ops:
  7.2 0.0 copy-start
  7.2 0.0 copy-start.1
  7.2 0.0 all-gather.7.cloned.1.call-start
  7.2 52.5 %pool.1 = (bf16[64,128,128]{2,1,0:T(8,128)(2,1)}, bf16[32,256,128]{2,1,0:T(8,128)(2,1)}) custom-call(s32[32768]{0:T(1024)} %bitcast.34, s32[128,128]{1,0:T(8,128)} %bitcast.31, s32[32,256]{1,0:T(8,128)} %bitcast.36, bf16[8192,128]{1,0:T(8,128)(2,1)} %bitcast.25, bf16[32,512,128]{2,1,0:T(8,128)(2,1)} %small_far.1), custom_call_target="tpu_custom_call" | custom-call | bytes 96000000 | tf_op jit(solution)/shard_map/pool/pallas_call | solution.py:168
  59.7 0.0 all-gather.7.cloned.1.call-update
  59.7 0.0 copy-done.1
  59.8 0.8 copy.14.labels
  60.6 0.0 copy-done
  60.6 0.7 dynamic-slice_reduce_fusion.sizes
  61.3 46.4 %top.1 = (bf16[32,256,128]{2,1,0:T(8,128)(2,1)}, bf16[2,64,128,128]{3,2,1,0:T(8,128)(2,1)}) custom-call(s32[64]{0:T(128)} %dynamic-slice_reduce_fusion.sizes, bf16[64,128,128]{2,1,0:T(8,128)(2,1)} %get-tuple-element.10.arrived, bf16[32,256,128]{2,1,0:T(8,128)(2,1)} %get-tuple-element.11.small, bf16[256,128]{1,0:T(8,128)(2,1)} %dense.1, ...), custom_call_target="tpu_custom_call" | custom-call | bytes 135000000 | tf_op jit(solution)/shard_map/top/pallas_call | solution.py:441
  107.6 7.1 %all-to-all-start = ((bf16[32,256,128]{2,1,0:T(8,128)(2,1)}), bf16[32,256,128]{2,1,0:T(8,128)(2,1)S(1)}, u32[]{:S(2)}, u32[]{:S(2)}) async-start(bf16[32,256,128]{2,1,0:T(8,128)(2,1)} %get-tuple-element.12), calls=%async_computation | async-start | bytes 4194304 | tf_op jit(solution)/shard_map/all_to_all | solution.py:493
  114.7 0.0 all-gather.5.cloned.1.call-start
  114.8 2.0 all-gather.7.cloned.1.call-done
  116.8 1.0 constant_dynamic-slice_fusion
  117.8 27.5 %all-to-all-done = bf16[32,256,128]{2,1,0:T(8,128)(2,1)S(1)} async-done(((bf16[32,256,128]{2,1,0:T(8,128)(2,1)}), bf16[32,256,128]{2,1,0:T(8,128)(2,1)S(1)}, u32[]{:S(2)}, u32[]{:S(2)}) %all-to-all-start) | async-done | bytes 2097184 | tf_op jit(solution)/shard_map/all_to_all | solution.py:493
  145.3 5.6 %fusion.2 = bf16[512,128]{1,0:T(8,128)(2,1)S(1)} fusion(bf16[8192,128]{1,0:T(8,128)(2,1)S(1)} %bitcast.29, s32[8192]{0:T(1024)S(1)} %bitcast.38), kind=kOutput, calls=%fused_computation.3 | convolution fusion | flops 1078001664 | bytes 2260992 | tf_op jit(solution)/shard_map/sr,se->re/dot_general | solution.py:495
  150.9 10.2 %all-gather.1 = bf16[2048,128]{1,0:T(8,128)(2,1)S(1)} all-gather(bf16[512,128]{1,0:T(8,128)(2,1)S(1)} %fusion.2), channel_id=3, replica_groups=mesh['rep'=2,'y'=4,'zl'=2,'x'=4,'core'=2] {'x'}, dimensions={0}, use_global_device_ids=true | all-gather | bytes 655360 | tf_op jit(solution)/shard_map/all_gather | solution.py:496
  161.1 0.1 convert_reduce_fusion
  161.1 1.6 fusion.3
  162.7 0.0 all-gather.5.cloned.1.call-update
  162.8 62.8 %all_to_all.10.folds = bf16[128,128,128]{2,1,0:T(8,128)(2,1)} all-to-all(bf16[128,128,128]{2,1,0:T(8,128)(2,1)} %bitcast.27), channel_id=1, replica_groups=mesh['rep'=2,'y'=4,'zl'=2,'x'=4,'core'=2] {'rep','y','zl','x','core'}, dimensions={0} | all-to-all | bytes 8388608 | tf_op jit(solution)/shard_map/all_to_all | solution.py:503
  225.6 37.0 %scatter.1 = bf16[8192,128]{1,0:T(8,128)(2,1)} custom-call(s32[32768]{0:T(1024)} %bitcast.35, s32[16384]{0:T(1024)} %bitcast.33, s32[128,128]{1,0:T(8,128)} %bitcast.32, bf16[128,128,128]{2,1,0:T(8,128)(2,1)} %all_to_all.10.folds, bf16[8192,128]{1,0:T(8,128)(2,1)} %bitcast.26), custom_call_target="tpu_custom_call" | custom-call | bytes 84000000 | tf_op jit(solution)/shard_map/scatter/pallas_call | solution.py:252
  262.6 0.1 all-gather.5.cloned.1.call-done
  262.7 4.7 %copy.16 = bf16[32,512,128]{2,1,0:T(8,128)(2,1)} copy(bf16[32,512,128]{2,1,0:T(8,128)(2,1)} %all-gather.5.cloned.1.call-done) | data formatting | bytes 8388608
Async XLA Ops:
  7.2 53.4 %copy-start = (s32[64,128]{1,0:T(8,128)S(1)}, s32[64,128]{1,0:T(8,128)}, u32[]{:S(2)}) copy-start(s32[64,128]{1,0:T(8,128)} %param.16) | copy-start | bytes 98308
  7.2 52.6 %copy-start.1 = (s32[256]{0:T(256)S(1)}, s32[256]{0:T(256)}, u32[]{:S(2)}) copy-start(s32[256]{0:T(256)} %param.13) | copy-start | bytes 3076
  7.2 109.6 %all-gather.7.cloned.1.call-start = ((), (), s32[]{:S(2)}) async-start(), calls=%async_computation.3 | async-start | bytes 1081344 | tf_op jit(solution)/shard_map/all_gather | solution.py:487
  107.6 37.6 %all-to-all-start = ((bf16[32,256,128]{2,1,0:T(8,128)(2,1)}), bf16[32,256,128]{2,1,0:T(8,128)(2,1)S(1)}, u32[]{:S(2)}, u32[]{:S(2)}) async-start(bf16[32,256,128]{2,1,0:T(8,128)(2,1)} %get-tuple-element.12), calls=%async_computation | async-start | bytes 4194304 | tf_op jit(solution)/shard_map/all_to_all | solution.py:493
  114.7 147.9 %all-gather.5.cloned.1.call-start = ((), (), s32[]{:S(2)}) async-start(), calls=%async_computation.2 | async-start | bytes 4325376 | tf_op jit(solution)/shard_map/all_gather | solution.py:501
Sparse Core Ops, SparseCore 0:
  59.8 56.9 all-gather.6
  162.9 99.7 all-gather.4
